TPU v7x, 1024 devices: a whole 4x4x32 slice. The times are simulated.
1024 devices in a mesh: grp: 16 (over y, x), wide: 64 (over z, core).
Axes of the slice: x: 4, y: 4, z: 32, core: 2. Of those that a mesh axis runs over, the one named last changes fastest.
Arguments:
- sequences: bfloat16 [1024, 128, 512], P(('grp', 'wide')), may hold values from -6 to 6
- upstream: bfloat16 [1024, 128, 512], P(('grp', 'wide')), may hold values from -6 to 6
- lengths: int32 [16, 64, 1], P('grp'), may hold values from 16 to 128
- swap_table: int32 [16, 32, 1], P('grp'), may hold values from 0 to 1
- input_weight: bfloat16 [512, 2048], replicated, may hold values from -0.25 to 0.25
- output_weight: bfloat16 [512, 512], replicated, may hold values from -0.25 to 0.25
Outputs:
- layer_out: bfloat16 [1024, 128, 512], P(('grp', 'wide'))
- input_grad: bfloat16 [1024, 128, 512], P(('grp', 'wide'))
- input_weight_gradient: float32 [512, 2048], P('wide')
- output_weight_gradient: float32 [512, 512], P('wide')
All inputs are finite; a program needn't handle non-finite values.
Results may differ from a plain program's by a relative error of at most 0.018.
Values may be sent and summed in bfloat16 or wider, within the bound.
No kernel may reach another device: no remote copies, remote signals or barrier semaphores. Data moves between devices by JAX's collectives and lax.ppermute only.
A program may use at most 64 MiB of HBM per device.

v0:
```python
import math

import jax
import jax.numpy as jnp
from jax import lax
from jax.sharding import PartitionSpec as P

HEADS = 8
HEAD_DIM = 64
SEQ_DEV = 1
LEN = 128


epsilon = 1e-06


def shortened(x):

    def short(part):
        return part.astype(jnp.bfloat16) if part.dtype == jnp.float32 else part

    return jax.tree.map(short, x)


def from_behind(block, axis, distance):
    devices = range(lax.axis_size(axis))
    route = [((i - distance) % len(devices), i) for i in devices]
    return lax.ppermute(block, axis, route)


def cut_along(x, dim, size):
    before, after = (x.shape[:dim], x.shape[dim + 1 :])
    return jnp.moveaxis(x.reshape(*before, size, -1, *after), dim, 0)


def sum_packed(arrays, axis, dims):
    size = lax.axis_size(axis)
    parts = [cut_along(a, dim, size) for a, dim in zip(arrays, dims)]
    lines = jnp.concatenate([b.reshape(size, -1) for b in parts], axis=1)
    span = max(16, -(-lines.shape[1] // 1024) * 8)
    lines = jnp.pad(lines, ((0, 0), (0, span * 128 - lines.shape[1]))).reshape(-1, 128)
    ravelled, at, outs = (lax.psum_scatter(lines, axis, tiled=True).reshape(-1), 0, [])
    for b in parts:
        part = b[0]
        outs.append(ravelled[at : at + part.size].reshape(part.shape))
        at += part.size
    return tuple(outs)


def sent_to_all(x, axis):
    copies = jnp.broadcast_to(x, (lax.axis_size(axis), *x.shape))
    return lax.all_to_all(copies, axis, split_axis=0, concat_axis=0, tiled=True)


def over_copies(x, axis):
    return sent_to_all(x, axis).astype(jnp.float32).sum(axis=0)


def normalize(values):
    return values * lax.rsqrt(jnp.mean(values * values, axis=-1, keepdims=True) + epsilon)


def layer_grads(rows, cotangent, lengths, input_weight, output_weight):
    slots, length_rows, width = rows.shape
    positions = jnp.arange(length_rows, dtype=jnp.int32)
    valid_rows = positions[None, :] < lengths[:, None]
    allowed = (positions[:, None] >= positions[None, :])[None, None] & valid_rows[:, None, None, :]
    input_single_precision = rows.astype(jnp.float32)
    norm_result_input = normalize(input_single_precision).astype(jnp.bfloat16)
    hidden_state = jnp.einsum(
        "xbg,gm->xbm", norm_result_input, input_weight, preferred_element_type=jnp.float32
    )

    def post(hidden_state, input_single_precision):
        activated = jax.nn.silu(hidden_state).astype(jnp.bfloat16)
        gate_part = activated[..., :width]
        value_part = activated[..., width : 2 * width].reshape(slots, length_rows, HEADS, HEAD_DIM)
        query_part = activated[..., 2 * width : 3 * width].reshape(
            slots, length_rows, HEADS, HEAD_DIM
        )
        key_part = activated[..., 3 * width :].reshape(slots, length_rows, HEADS, HEAD_DIM)
        scores = jnp.einsum(
            "sqhc,skhc->shqk", query_part, key_part, preferred_element_type=jnp.float32
        ) * HEAD_DIM ** (-0.5)
        weights = jnp.where(allowed, jax.nn.silu(scores), 0.0).astype(jnp.bfloat16)
        attended = jnp.einsum(
            "shqk,skhc->sqhc", weights, value_part, preferred_element_type=jnp.float32
        ).reshape(slots, length_rows, width)
        gate_applied = (gate_part * normalize(attended)).astype(jnp.bfloat16)
        layer_result = input_single_precision + jnp.einsum(
            "xbg,gm->xbm", gate_applied, output_weight, preferred_element_type=jnp.float32
        )
        return (layer_result.astype(jnp.bfloat16), gate_applied)

    layer_result, pull_back, gate_applied = jax.vjp(
        post, hidden_state, input_single_precision, has_aux=True
    )
    mask_applied = cotangent * valid_rows[..., None].astype(cotangent.dtype)
    hidden_state_gradient, direct_grad = pull_back(mask_applied)
    hidden_state_gradient = hidden_state_gradient.astype(jnp.bfloat16)
    norm_result_gradient = jnp.einsum(
        "wmo,bo->wmb", hidden_state_gradient, input_weight, preferred_element_type=jnp.float32
    )
    _, norm_back = jax.vjp(normalize, input_single_precision)
    input_grad = (direct_grad + norm_back(norm_result_gradient)[0]).astype(jnp.bfloat16)
    input_weight_gradient = jnp.einsum(
        "uwn,uwo->no", norm_result_input, hidden_state_gradient, preferred_element_type=jnp.float32
    )
    output_weight_gradient = jnp.einsum(
        "uwn,uwo->no", gate_applied, mask_applied, preferred_element_type=jnp.float32
    )
    return (layer_result, input_grad, input_weight_gradient, output_weight_gradient)


def body(sequences, upstream, lengths, swap_table, input_weight, output_weight):
    axis_width = lax.axis_size("wide")
    half_width = axis_width // 2
    position = lax.axis_index("wide")
    pair_slot = position % half_width
    swap_flags = lax.dynamic_index_in_dim(swap_table[0], pair_slot, 0, keepdims=False)
    own_lengths = lax.dynamic_index_in_dim(lengths[0], position, 0, keepdims=False)
    chosen = (swap_flags == 1)[:, None, None]
    home_out, input_grad, input_weight_gradient, output_weight_gradient = layer_grads(
        sequences, upstream, own_lengths, input_weight, output_weight
    )
    arrived = jax.tree.map(
        lambda part, own: part.astype(own.dtype),
        from_behind(shortened(home_out), "wide", half_width),
        home_out,
    )
    layer_out = jnp.where(chosen, arrived, home_out)
    grad_scale = 1.0 / math.sqrt(SEQ_DEV * LEN * axis_width * lax.axis_size("grp"))
    input_weight_gradient = input_weight_gradient * grad_scale
    output_weight_gradient = output_weight_gradient * grad_scale
    shares = sum_packed((input_weight_gradient, output_weight_gradient), "wide", (0, 0))
    total_in, total_out = (
        over_copies(shares[0].astype(jnp.bfloat16), "grp").astype(jnp.float32),
        over_copies(shares[1].astype(jnp.bfloat16), "grp").astype(jnp.float32),
    )
    return (layer_out, input_grad, total_in, total_out)


def solution(mesh):
    placed = (
        P(("grp", "wide"), None, None),
        P(("grp", "wide"), None, None),
        P("grp", None, None),
        P("grp", None, None),
        P(),
        P(),
    )
    return jax.shard_map(
        body,
        mesh=mesh,
        in_specs=placed,
        out_specs=(
            P(("grp", "wide"), None, None),
            P(("grp", "wide"), None, None),
            P("wide", None),
            P("wide", None),
        ),
        check_vma=False,
    )
```

profile of v0, /device:TPU:2, one launch (start us, length us, event | category | flops | bytes accessed | tf_op | source)
XLA Modules:
  0.0 335.0 jit_solution(6714283013230679314)
XLA Ops:
  7.2 1.2 fusion.19
  8.9 1.2 constant_dynamic-slice_fusion
  10.2 1.2 iota_compare_fusion.1
  11.4 1.4 fusion.34
  12.8 1.0 copy-done.1
  15.1 1.2 select_convert_fusion
  16.3 1.3 fusion.22
  18.4 1.4 fusion.4
  19.7 1.4 multiply_reduce_fusion
  21.8 1.4 add_add_fusion.1
  23.2 1.1 copy.39
  24.3 1.8 fusion.43
  26.2 1.6 fusion.11
  29.0 1.7 copy.42
  31.4 1.7 copy.41
  33.2 1.4 fusion.23
  34.6 2.0 convolution_multiply_fusion.1
  36.6 1.4 reshape_reshape.7
  38.0 4.2 %convolution_multiply_fusion = f32[512,2048]{1,0:T(8,128)} fusion(bf16[1,128,512]{2,1,0:T(8,128)(2,1)S(1)} %copy-done.3, f32[128]{0:T(128)S(1)} %copy-done.14, f32[128,2048]{1,0:T(8,128)} %copy-done.1, bf16[1,128,512]{2,1,0:T(8,128)(2,1)} %fusion.23, bf16[1,128,512]{2,1,0:T(8,128)(2,1)} %copy.42, bf16[1,128,512]{2,1,0:T(8,128)(2,1)} %copy.41, ...), kind=kOutput, calls=%fused_computation.1 | convolution fusion | flops 274399232 | bytes 5898752 | tf_op jit(solution)/shard_map/uwn,uwo->no/dot_general | solution.py:106
  42.2 5.0 %reshape_reshape.6 = f32[64,16384]{1,0:T(8,128)} reshape(f32[512,2048]{1,0:T(8,128)} %convolution_multiply_fusion) | data formatting | bytes 8388608 | tf_op jit(solution)/shard_map/reshape;reshape | solution.py:39
  47.1 4.9 %pad_maximum_fusion = f32[64,20480]{1,0:T(8,128)} fusion(f32[64,4096]{1,0:T(8,128)S(1)} %reshape_reshape.7, f32[64,16384]{1,0:T(8,128)} %reshape_reshape.6), kind=kLoop, calls=%fused_computation | loop fusion | flops 1310720 | bytes 10485760 | tf_op jit(solution)/shard_map/concatenate | solution.py:39
  52.0 5.5 %reshape.324 = f32[10240,128]{1,0:T(8,128)} reshape(f32[64,20480]{1,0:T(8,128)} %pad_maximum_fusion) | data formatting | bytes 10485760 | tf_op jit(solution)/shard_map/reshape | solution.py:41
  57.6 2.0 fusion.3
  59.6 29.0 %collective-permute-start = (bf16[1,128,512]{2,1,0:T(8,128)(2,1)}, bf16[1,128,512]{2,1,0:T(8,128)(2,1)}, u32[]{:S(2)}, u32[]{:S(2)}) collective-permute-start(bf16[1,128,512]{2,1,0:T(8,128)(2,1)} %fusion.3), channel_id=1, source_target_pairs={{32,0},{33,1},{34,2},{35,3},{36,4},{37,5},{38,6},{39,7},{40,8},{41... | collective-permute-start | bytes 393224 | tf_op jit(solution)/shard_map/ppermute | solution.py:28
  89.2 2.7 fusion.21
  91.9 204.9 %reduce-scatter.2.cloned.1.call-done = f32[160,128]{1,0:T(8,128)} async-done(((f32[10240,128]{1,0:T(8,128)}), f32[160,128]{1,0:T(8,128)}) %reduce-scatter.2.cloned.1.call-update) | async-done | bytes 81936 | tf_op jit(solution)/shard_map/reduce_scatter | solution.py:42
  298.5 7.5 %all-to-all-start.1 = ((bf16[16,8,512]{2,1,0:T(8,128)(2,1)}), bf16[16,8,512]{2,1,0:T(8,128)(2,1)S(1)}, u32[]{:S(2)}, u32[]{:S(2)}) async-start(bf16[16,8,512]{2,1,0:T(8,128)(2,1)} %broadcast_in_dim.56), calls=%async_computation.2 | async-start | bytes 262144 | tf_op jit(solution)/shard_map/all_to_all | solution.py:52
  306.0 6.6 %all-to-all-done.1 = bf16[16,8,512]{2,1,0:T(8,128)(2,1)S(1)} async-done(((bf16[16,8,512]{2,1,0:T(8,128)(2,1)}), bf16[16,8,512]{2,1,0:T(8,128)(2,1)S(1)}, u32[]{:S(2)}, u32[]{:S(2)}) %all-to-all-start.1) | async-done | bytes 131104 | tf_op jit(solution)/shard_map/all_to_all | solution.py:52
  313.4 4.8 %all-to-all-start = ((bf16[16,8,2048]{2,1,0:T(8,128)(2,1)}), bf16[16,8,2048]{2,1,0:T(8,128)(2,1)S(1)}, u32[]{:S(2)}, u32[]{:S(2)}) async-start(bf16[16,8,2048]{2,1,0:T(8,128)(2,1)} %broadcast_in_dim.55), calls=%async_computation.1 | async-start | bytes 1048576 | tf_op jit(solution)/shard_map/all_to_all | solution.py:52
  318.2 1.8 fusion.18
  320.0 2.2 broadcast_select_fusion
  322.9 4.6 %all-to-all-done = bf16[16,8,2048]{2,1,0:T(8,128)(2,1)S(1)} async-done(((bf16[16,8,2048]{2,1,0:T(8,128)(2,1)}), bf16[16,8,2048]{2,1,0:T(8,128)(2,1)S(1)}, u32[]{:S(2)}, u32[]{:S(2)}) %all-to-all-start) | async-done | bytes 524320 | tf_op jit(solution)/shard_map/all_to_all | solution.py:52
  (65 shorter events, 9.8 us)
Async XLA Ops:
  7.2 4.2 %copy-start = (bf16[512,2048]{1,0:T(8,128)(2,1)S(1)}, bf16[512,2048]{1,0:T(8,128)(2,1)}, u32[]{:S(2)}) copy-start(bf16[512,2048]{1,0:T(8,128)(2,1)} %param.10) | copy-start | bytes 6291460
  7.2 289.7 %reduce-scatter.2.cloned.1.call-start = ((), (), s32[]{:S(2)}) async-start(), calls=%async_computation.3 | async-start | bytes 5324800 | tf_op jit(solution)/shard_map/reduce_scatter | solution.py:42
  8.4 0.5 copy-start.15
  8.9 5.2 %copy-start.13 = (f32[128]{0:T(128)}, f32[128]{0:T(128)S(1)}, u32[]{:S(2)}) copy-start(f32[128]{0:T(128)S(1)} %fusion.36) | copy-start | bytes 1540
  12.8 1.0 copy-start.1
  13.8 4.6 %copy-start.4 = (bf16[1,128,512]{2,1,0:T(8,128)(2,1)S(1)}, bf16[1,128,512]{2,1,0:T(8,128)(2,1)}, u32[]{:S(2)}) copy-start(bf16[1,128,512]{2,1,0:T(8,128)(2,1)} %param.7) | copy-start | bytes 393220
  14.2 4.1 %copy-start.7 = (bf16[1,128,512]{1,2,0:T(8,128)(2,1)}, bf16[1,128,512]{1,2,0:T(8,128)(2,1)S(1)}, u32[]{:S(2)}) copy-start(bf16[1,128,512]{1,2,0:T(8,128)(2,1)S(1)} %copy.35) | copy-start | bytes 393220
  14.4 4.0 %copy-start.9 = (bf16[1,128,512]{1,2,0:T(8,128)(2,1)}, bf16[1,128,512]{1,2,0:T(8,128)(2,1)S(1)}, u32[]{:S(2)}) copy-start(bf16[1,128,512]{1,2,0:T(8,128)(2,1)S(1)} %copy.34) | copy-start | bytes 393220
  16.3 1.8 copy-start.6
  17.6 0.6 copy-start.17
  23.2 4.6 %copy-start.8 = (bf16[1,128,512]{1,2,0:T(8,128)(2,1)S(1)}, bf16[1,128,512]{1,2,0:T(8,128)(2,1)}, u32[]{:S(2)}) copy-start(bf16[1,128,512]{1,2,0:T(8,128)(2,1)} %copy-done.7) | copy-start | bytes 393220
  23.2 5.5 %copy-start.10 = (bf16[1,128,512]{1,2,0:T(8,128)(2,1)S(1)}, bf16[1,128,512]{1,2,0:T(8,128)(2,1)}, u32[]{:S(2)}) copy-start(bf16[1,128,512]{1,2,0:T(8,128)(2,1)} %copy-done.9) | copy-start | bytes 393220
  23.2 11.3 %copy-start.5 = (bf16[128,512]{1,0:T(8,128)(2,1)S(1)}, bf16[128,512]{1,0:T(8,128)(2,1)}, u32[]{:S(2)}) copy-start(bf16[128,512]{1,0:T(8,128)(2,1)} %get-tuple-element.5) | copy-start | bytes 393220
  24.3 1.9 copy-start.11
  26.2 11.8 %copy-start.3 = (bf16[1,128,512]{2,1,0:T(8,128)(2,1)S(1)}, bf16[1,128,512]{2,1,0:T(8,128)(2,1)}, u32[]{:S(2)}) copy-start(bf16[1,128,512]{2,1,0:T(8,128)(2,1)} %param.6) | copy-start | bytes 393220
  27.8 10.2 %copy-start.14 = (f32[128]{0:T(128)S(1)}, f32[128]{0:T(128)}, u32[]{:S(2)}) copy-start(f32[128]{0:T(128)} %copy-done.13) | copy-start | bytes 1540
  57.6 31.0 %copy-start.18 = (s32[1,32,1]{1,2,0:T(1,128)S(1)}, s32[1,32,1]{1,2,0:T(1,128)}, u32[]{:S(2)}) copy-start(s32[1,32,1]{1,2,0:T(1,128)} %param.9) | copy-start | bytes 388
  57.6 31.6 %copy-start.2 = (f32[128,2048]{1,0:T(8,128)S(1)}, f32[128,2048]{1,0:T(8,128)}, u32[]{:S(2)}) copy-start(f32[128,2048]{1,0:T(8,128)} %copy-done.1) | copy-start | bytes 3145732
  59.6 260.4 %collective-permute-start = (bf16[1,128,512]{2,1,0:T(8,128)(2,1)}, bf16[1,128,512]{2,1,0:T(8,128)(2,1)}, u32[]{:S(2)}, u32[]{:S(2)}) collective-permute-start(bf16[1,128,512]{2,1,0:T(8,128)(2,1)} %fusion.3), channel_id=1, source_target_pairs={{32,0},{33,1},{34,2},{35,3},{36,4},{37,5},{38,6},{39,7},{40,8},{41... | collective-permute-start | bytes 393224 | tf_op jit(solution)/shard_map/ppermute | solution.py:28
  89.2 216.7 %copy-start.16 = (f32[128]{0:T(128)S(1)}, f32[128]{0:T(128)}, u32[]{:S(2)}) copy-start(f32[128]{0:T(128)} %copy-done.15) | copy-start | bytes 1540
  89.2 229.0 %copy-start.12 = (bf16[128]{0:T(256)(128)(2,1)S(1)}, bf16[128]{0:T(256)(128)(2,1)}, u32[]{:S(2)}) copy-start(bf16[128]{0:T(256)(128)(2,1)} %get-tuple-element.16) | copy-start | bytes 772
  298.5 14.1 %all-to-all-start.1 = ((bf16[16,8,512]{2,1,0:T(8,128)(2,1)}), bf16[16,8,512]{2,1,0:T(8,128)(2,1)S(1)}, u32[]{:S(2)}, u32[]{:S(2)}) async-start(bf16[16,8,512]{2,1,0:T(8,128)(2,1)} %broadcast_in_dim.56), calls=%async_computation.2 | async-start | bytes 262144 | tf_op jit(solution)/shard_map/all_to_all | solution.py:52
  313.4 14.0 %all-to-all-start = ((bf16[16,8,2048]{2,1,0:T(8,128)(2,1)}), bf16[16,8,2048]{2,1,0:T(8,128)(2,1)S(1)}, u32[]{:S(2)}, u32[]{:S(2)}) async-start(bf16[16,8,2048]{2,1,0:T(8,128)(2,1)} %broadcast_in_dim.55), calls=%async_computation.1 | async-start | bytes 1048576 | tf_op jit(solution)/shard_map/all_to_all | solution.py:52
Sparse Core Ops, SparseCore 0:
  57.7 239.0 reduce-scatter.1
where the time goes:
time: 336 us; the launch traced here: 335 us
  waiting for transfers between devices  216 us (64%)
  starting transfers between devices  41.3 us (12%)
  local copies, waits for them, and re-layouts  22.8 us (7%)
  matrix products  20.7 us (6%)
  other arithmetic  19.8 us (6%)
  between operations  14.3 us (4%)
    reduce_scatter x1, waiting for transfers between devices, sum_packed(): lax.psum_scatter(lines, axis, tiled=True).reshape(-1)  205 us
    ppermute x1, starting transfers between devices, from_behind(): return lax.ppermute(block, axis, route)  29 us
    all_to_all x2, starting transfers between devices, sent_to_all(): return lax.all_to_all(copies, axis, split_axis=0, concat_axis=0, tiled=True)  12.3 us
    all_to_all x2, waiting for transfers between devices, sent_to_all(): return lax.all_to_all(copies, axis, split_axis=0, concat_axis=0, tiled=True)  11.1 us
  transfers between devices with their start and end apart: 4, of which 3 were waited for; matrix products, arithmetic and copies ran while one was open for 4% of the time, Pallas kernels for 0%

commit v1 on v0

v1 whole, which is shorter than its diff:
```python
import math

import jax
import jax.numpy as jnp
from jax import lax
from jax.experimental import pallas as pl
from jax.experimental.pallas import tpu as pltpu
from jax.sharding import PartitionSpec as P

HEADS = 8
HEAD_DIM = 64
LEN = 128
D = 512
GROUPS = 16
CHIPS = 32
CORES = 2
ROWS = 320
epsilon = 1e-06
f32 = jnp.float32
bf16 = jnp.bfloat16


def nn(a, b):
    return lax.dot_general(a, b, (((1,), (0,)), ((), ())), preferred_element_type=f32)


def nt(a, b):
    return lax.dot_general(a, b, (((1,), (1,)), ((), ())), preferred_element_type=f32)


def tn(a, b):
    return lax.dot_general(a, b, (((0,), (0,)), ((), ())), preferred_element_type=f32)


def sigmoid(x):
    return 0.5 * jnp.tanh(0.5 * x) + 0.5


def layer_kernel(
    lengths_ref,
    x_ref,
    up_ref,
    win_ref,
    wout_ref,
    home_ref,
    xgrad_ref,
    send_ref,
    keep_ref,
    act_ref,
    slope_ref,
    wslope_ref,
    weights_ref,
    hgrad_ref,
    normed_t,
    gated_t,
):
    position = lax.axis_index("wide")
    length = lengths_ref[position]
    core = lax.rem(position, 2)
    x = x_ref[0].astype(f32)
    inverse = lax.rsqrt(jnp.mean(x * x, axis=-1, keepdims=True) + epsilon)
    unit = x * inverse
    normed = unit.astype(bf16)
    normed_t[...] = unit.astype(bf16).astype(f32).T.reshape(CHIPS, 16, LEN)
    for part in range(4):
        columns = pl.ds(part * D, D)
        hidden = nn(normed, win_ref[:, columns])
        sig = sigmoid(hidden)
        activated = hidden * sig
        act_ref[:, columns] = activated.astype(bf16)
        slope_ref[:, columns] = sig + activated * (1.0 - sig)

    query_at = lax.broadcasted_iota(jnp.int32, (LEN, LEN), 0)
    key_at = lax.broadcasted_iota(jnp.int32, (LEN, LEN), 1)
    allowed = (key_at <= query_at) & (key_at < length)
    first = lax.broadcasted_iota(jnp.int32, (LEN, LEN), 1) < HEAD_DIM

    def by_head(block):
        wide = block.astype(f32)
        return (
            jnp.where(first, wide, 0.0).astype(bf16),
            jnp.where(first, 0.0, wide).astype(bf16),
        )

    attended = []
    for pair in range(HEADS // 2):
        at = pair * 128
        queries = by_head(act_ref[:, 2 * D + at : 2 * D + at + 128])
        keys = act_ref[:, 3 * D + at : 3 * D + at + 128]
        values = by_head(act_ref[:, D + at : D + at + 128])
        for side in range(2):
            scores = nt(queries[side], keys) * HEAD_DIM**-0.5
            sig = sigmoid(scores)
            smooth = scores * sig
            slope = (sig + smooth * (1.0 - sig)) * HEAD_DIM**-0.5
            wslope_ref[2 * pair + side] = jnp.where(allowed, slope, 0.0)
            weights_ref[pair, side * LEN : (side + 1) * LEN, :] = jnp.where(
                allowed, smooth, 0.0
            ).astype(bf16)
        attended.append(
            nn(weights_ref[pair, :LEN, :], values[0]) + nn(weights_ref[pair, LEN:, :], values[1])
        )
    attended = jnp.concatenate(attended, axis=1)
    spread = lax.rsqrt(jnp.mean(attended * attended, axis=-1, keepdims=True) + epsilon)
    unit_attended = attended * spread
    gate = act_ref[:, :D].astype(f32)
    gated = (gate * unit_attended).astype(bf16)
    gated_t[...] = gated.astype(f32).T
    home_ref[0] = (x + nn(gated, wout_ref[...])).astype(bf16)

    alive = lax.broadcasted_iota(jnp.int32, (LEN, D), 0) < length
    masked_wide = jnp.where(alive, up_ref[0].astype(f32), 0.0)
    masked = masked_wide.astype(bf16)
    gated_grad = nt(masked, wout_ref[...]).astype(bf16).astype(f32)
    hgrad_ref[:, :D] = (
        (gated_grad * unit_attended).astype(bf16).astype(f32) * slope_ref[:, :D]
    ).astype(bf16)
    unit_grad = gated_grad * gate
    overlap = jnp.mean(unit_grad * unit_attended, axis=-1, keepdims=True)
    attended_grad = spread * (unit_grad - unit_attended * overlap)

    for pair in range(HEADS // 2):
        at = pair * 128
        queries = by_head(act_ref[:, 2 * D + at : 2 * D + at + 128])
        keys = by_head(act_ref[:, 3 * D + at : 3 * D + at + 128])
        values = act_ref[:, D + at : D + at + 128]
        grads = by_head(attended_grad[:, at : at + 128])
        both = jnp.concatenate(grads, axis=0)
        weight_grads = nt(both, values)
        value_grad = tn(weights_ref[pair], both)
        score_grads = (
            weight_grads * wslope_ref[2 * pair : 2 * pair + 2].reshape(2 * LEN, LEN)
        ).astype(bf16)
        query_grad = nn(score_grads[:LEN], keys[0]) + nn(score_grads[LEN:], keys[1])
        key_grad = tn(score_grads, jnp.concatenate(queries, axis=0))
        for start, grad in ((D, value_grad), (2 * D, query_grad), (3 * D, key_grad)):
            columns = pl.ds(start + at, 128)
            hgrad_ref[:, columns] = (grad * slope_ref[:, columns]).astype(bf16)

    unit_grad = nt(hgrad_ref[...], win_ref[...])
    overlap = jnp.mean(unit_grad * unit, axis=-1, keepdims=True)
    xgrad_ref[0] = (masked_wide + inverse * (unit_grad - unit * overlap)).astype(bf16)

    for out_ref, side in ((send_ref, 1 - core), (keep_ref, core)):
        mine = normed_t[:, pl.ds(pl.multiple_of(side * 8, 8), 8), :].reshape(256, LEN).astype(bf16)
        for block in range(4):
            grads = nn(mine, hgrad_ref[:, block * 512 : (block + 1) * 512]).astype(bf16)
            for j in range(4):
                out_ref[4 * block + j, 0:256, :] = grads[:, j * 128 : (j + 1) * 128]
        mine = jnp.concatenate(
            [gated_t[pl.ds(side * 8 + i, CHIPS, stride=16), :] for i in range(8)], axis=0
        ).astype(bf16)
        grads = nn(mine, masked).astype(bf16)
        for block in range(4):
            for p in range(4):
                out_ref[4 * block + p, 256:320, :] = grads[
                    p * 64 : (p + 1) * 64, block * 128 : (block + 1) * 128
                ]


def layer(lengths, x, up, win, wout):
    vmem = pl.BlockSpec(memory_space=pltpu.VMEM)
    smem = pl.BlockSpec(memory_space=pltpu.SMEM)
    block = jax.ShapeDtypeStruct((1, LEN, D), bf16)
    grads = jax.ShapeDtypeStruct((GROUPS, ROWS, 128), bf16)
    return pl.pallas_call(
        layer_kernel,
        out_shape=(block, block, grads, grads),
        in_specs=[smem, vmem, vmem, vmem, vmem],
        out_specs=(vmem, vmem, vmem, vmem),
        scratch_shapes=[
            pltpu.VMEM((LEN, 4 * D), bf16),
            pltpu.VMEM((LEN, 4 * D), f32),
            pltpu.VMEM((HEADS, LEN, LEN), f32),
            pltpu.VMEM((HEADS // 2, 2 * LEN, LEN), bf16),
            pltpu.VMEM((LEN, 4 * D), bf16),
            pltpu.VMEM((CHIPS, 16, LEN), f32),
            pltpu.VMEM((D, LEN), f32),
        ],
        compiler_params=pltpu.CompilerParams(vmem_limit_bytes=40 << 20),
        name="layer",
    )(lengths, x, up, win, wout)


def group_sum_kernel(parts_ref, out_ref, total):
    summed = parts_ref[0].astype(f32)
    for g in range(1, GROUPS):
        summed += parts_ref[g].astype(f32)
    total[...] = summed
    for z in range(CHIPS):
        out_ref[z, 0:8, :] = total[8 * z : 8 * z + 8, :].astype(bf16)
        out_ref[z, 8:10, :] = total[pl.ds(256 + z, 2, stride=CHIPS), :].astype(bf16)


def group_sum(parts):
    vmem = pl.BlockSpec(memory_space=pltpu.VMEM)
    return pl.pallas_call(
        group_sum_kernel,
        out_shape=jax.ShapeDtypeStruct((CHIPS, 10, 128), bf16),
        in_specs=[vmem],
        out_specs=vmem,
        scratch_shapes=[pltpu.VMEM((ROWS, 128), f32)],
        name="group_sum",
    )(parts)


def chip_sum_kernel(parts_ref, out_ref):
    summed = parts_ref[0].astype(f32)
    for z in range(1, CHIPS):
        summed += parts_ref[z].astype(f32)
    summed = summed.astype(bf16)
    for g in range(GROUPS):
        out_ref[g] = summed


def chip_sum(parts):
    vmem = pl.BlockSpec(memory_space=pltpu.VMEM)
    return pl.pallas_call(
        chip_sum_kernel,
        out_shape=jax.ShapeDtypeStruct((GROUPS, 10, 128), bf16),
        in_specs=[vmem],
        out_specs=vmem,
        name="chip_sum",
    )(parts)


def finish_kernel(scale, swap_ref, home_ref, arrived_ref, parts_ref, out_ref, din_ref, dout_ref):
    position = lax.axis_index("wide")
    chosen = swap_ref[lax.rem(position, CHIPS)] == 1

    @pl.when(chosen)
    def _():
        out_ref[...] = arrived_ref[...]

    @pl.when(jnp.logical_not(chosen))
    def _():
        out_ref[...] = home_ref[...]

    for g in range(GROUPS):
        piece = parts_ref[g].astype(f32) * scale
        din_ref[:, g * 128 : (g + 1) * 128] = piece[:8]
        block, pair = g // 4, g % 4
        dout_ref[2 * pair : 2 * pair + 2, block * 128 : (block + 1) * 128] = piece[8:10]


def finish(scale, swaps, home, arrived, parts):
    vmem = pl.BlockSpec(memory_space=pltpu.VMEM)
    smem = pl.BlockSpec(memory_space=pltpu.SMEM)
    return pl.pallas_call(
        lambda *refs: finish_kernel(scale, *refs),
        out_shape=(
            jax.ShapeDtypeStruct((1, LEN, D), bf16),
            jax.ShapeDtypeStruct((8, 4 * D), f32),
            jax.ShapeDtypeStruct((8, D), f32),
        ),
        in_specs=[smem, vmem, vmem, vmem],
        out_specs=(vmem, vmem, vmem),
        name="finish",
    )(swaps, home, arrived, parts)


def body(sequences, upstream, lengths, swap_table, input_weight, output_weight):
    wide = lax.axis_size("wide")
    half = wide // 2
    home, input_grad, send, keep = layer(
        lengths.reshape(wide), sequences, upstream, input_weight, output_weight
    )
    received = lax.ppermute(send, "wide", [(i, i ^ 1) for i in range(wide)])
    arrived = lax.ppermute(home, "wide", [(i, (i + half) % wide) for i in range(wide)])
    chip = (keep.astype(f32) + received.astype(f32)).astype(bf16)
    parts = lax.all_to_all(chip, "grp", 0, 0, tiled=True)
    same_core = [[2 * z + c for z in range(CHIPS)] for c in range(CORES)]
    parts = lax.all_to_all(
        group_sum(parts), "wide", 0, 0, tiled=True, axis_index_groups=same_core
    )
    parts = lax.all_to_all(chip_sum(parts), "grp", 0, 0, tiled=True)
    scale = 1.0 / math.sqrt(LEN * wide * lax.axis_size("grp"))
    layer_out, total_in, total_out = finish(
        scale, swap_table.reshape(half), home, arrived, parts
    )
    return (layer_out, input_grad, total_in, total_out)


def solution(mesh):
    placed = (
        P(("grp", "wide"), None, None),
        P(("grp", "wide"), None, None),
        P("grp", None, None),
        P("grp", None, None),
        P(),
        P(),
    )
    return jax.shard_map(
        body,
        mesh=mesh,
        in_specs=placed,
        out_specs=(
            P(("grp", "wide"), None, None),
            P(("grp", "wide"), None, None),
            P("wide", None),
            P("wide", None),
        ),
        check_vma=False,
    )
```

time: 336 us -> 139 us (0.41)
  the two profiles are of different devices: /device:TPU:2 before, /device:TPU:32 now
where the time goes in v1:
time: 139 us; the launch traced here: 138 us
  starting transfers between devices  54.9 us (39%)
  waiting for transfers between devices  37.7 us (27%)
  blocking collectives  27.2 us (20%)
  Pallas kernels  11 us (8%)
  local copies, waits for them, and re-layouts  6.37 us (5%)
    all_to_all x1, starting transfers between devices, body(): lax.all_to_all(group_sum(parts), 'wide', 0, 0, tiled=True, axis_index_gro...  28.6 us
    all_to_all x1, blocking collectives, body(): parts = lax.all_to_all(chip, 'grp', 0, 0, tiled=True)  27.2 us
    all_to_all x1, waiting for transfers between devices, body(): lax.all_to_all(group_sum(parts), 'wide', 0, 0, tiled=True, axis_index_gro...  27 us
    ppermute x1, starting transfers between devices, body(): lax.ppermute(home, 'wide', [(i, (i + half) % wide) for i in range(wide)])  20.8 us
    all_to_all x1, waiting for transfers between devices, body(): parts = lax.all_to_all(chip_sum(parts), 'grp', 0, 0, tiled=True)  7.65 us
    unnamed x18, local copies, waits for them, and re-layouts  6.37 us
    pallas_call x1, Pallas kernels, layer(): pl.pallas_call(layer_kernel, out_shape=(block, block, grads, grads), in_s...  5.51 us
    all_to_all x1, starting transfers between devices, body(): parts = lax.all_to_all(chip_sum(parts), 'grp', 0, 0, tiled=True)  3.56 us
  transfers between devices with their start and end apart: 4, of which 3 were waited for; matrix products, arithmetic and copies ran while one was open for 0% of the time, Pallas kernels for 1%

profile of v1, /device:TPU:32, one launch (start us, length us, event | category | flops | bytes accessed | tf_op | source)
XLA Modules:
  0.0 138.1 jit_solution(14575661036676233373)
XLA Ops:
  0.6 0.0 copy-start
  0.6 1.6 %copy-done = bf16[512,2048]{1,0:T(8,128)(2,1)S(1)} copy-done((bf16[512,2048]{1,0:T(8,128)(2,1)S(1)}, bf16[512,2048]{1,0:T(8,128)(2,1)}, u32[]{:S(2)}) %copy-start) | copy-done | bytes 2097176
  2.2 0.0 copy-start.1
  2.2 1.0 copy-done.1
  3.3 0.0 copy-start.2
  3.3 0.9 copy-done.2
  4.2 0.0 copy-start.3
  4.2 0.9 copy-done.3
  5.1 0.0 copy-start.5
  5.1 0.7 copy-done.5
  5.7 5.5 %layer.1 = (bf16[1,128,512]{2,1,0:T(8,128)(2,1)S(1)}, bf16[1,128,512]{2,1,0:T(8,128)(2,1)}, bf16[16,320,128]{2,1,0:T(8,128)(2,1)S(1)}, bf16[16,320,128]{2,1,0:T(8,128)(2,1)S(1)}) custom-call(s32[64]{0:T(128)S(1)} %bitcast.2, bf16[1,128,512]{2,1,0:T(8,128)(2,1)S(1)} %copy-done.2, bf16[1,128,512]{2,1,0:T(8,128)(2,1)S(1)} %copy-done.3, ...), custom_call_target="tpu_custom_call" | custom-call | tf_op jit(solution)/shard_map/layer/pallas_call | solution.py:166
  11.2 0.0 copy-start.4
  11.2 1.9 %collective-permute-start.1 = (bf16[16,320,128]{2,1,0:T(8,128)(2,1)S(1)}, bf16[16,320,128]{2,1,0:T(8,128)(2,1)S(1)}, u32[]{:S(2)}, u32[]{:S(2)}) collective-permute-start(bf16[16,320,128]{2,1,0:T(8,128)(2,1)S(1)} %get-tuple-element.13), channel_id=1, source_target_pairs={{0,1},{1,0},{2,3},{3,2},{4,5},{5,4},{6,7},{7,6},{8,9},{9,8},{10,11... | collective-permute-start | bytes 3932168 | tf_op jit(solution)/shard_map/ppermute | solution.py:268
  13.2 3.0 %collective-permute-done.1 = bf16[16,320,128]{2,1,0:T(8,128)(2,1)S(1)} collective-permute-done((bf16[16,320,128]{2,1,0:T(8,128)(2,1)S(1)}, bf16[16,320,128]{2,1,0:T(8,128)(2,1)S(1)}, u32[]{:S(2)}, u32[]{:S(2)}) %collective-permute-start.1) | collective-permute-done | bytes 1310752 | tf_op jit(solution)/shard_map/ppermute | solution.py:268
  16.2 0.3 add_convert_fusion
  16.5 27.2 %all_to_all.15.parts_ref = bf16[16,320,128]{2,1,0:T(8,128)(2,1)} all-to-all(bf16[16,320,128]{2,1,0:T(8,128)(2,1)S(1)} %add_convert_fusion), channel_id=1, replica_groups=mesh['grp'=16,'wide'=64] {'grp'}, dimensions={0} | all-to-all | bytes 2621440 | tf_op jit(solution)/shard_map/all_to_all | solution.py:271
  43.7 2.2 %group_sum.1 = bf16[32,10,128]{2,1,0:T(8,128)(2,1)} custom-call(bf16[16,320,128]{2,1,0:T(8,128)(2,1)} %all_to_all.15.parts_ref), custom_call_target="tpu_custom_call" | custom-call | tf_op jit(solution)/shard_map/group_sum/pallas_call | solution.py:197
  45.9 28.6 %all-to-all-start.1 = ((bf16[32,10,128]{2,1,0:T(8,128)(2,1)}), bf16[32,10,128]{2,1,0:T(8,128)(2,1)S(1)}, u32[]{:S(2)}, u32[]{:S(2)}) async-start(bf16[32,10,128]{2,1,0:T(8,128)(2,1)} %group_sum.1), calls=%async_computation.1 | async-start | bytes 262144 | tf_op jit(solution)/shard_map/all_to_all | solution.py:273
  74.5 0.0 copy-done.4
  74.5 20.8 %collective-permute-start = (bf16[1,128,512]{2,1,0:T(8,128)(2,1)S(1)}, bf16[1,128,512]{2,1,0:T(8,128)(2,1)S(1)}, u32[]{:S(2)}, u32[]{:S(2)}) collective-permute-start(bf16[1,128,512]{2,1,0:T(8,128)(2,1)S(1)} %get-tuple-element.11.refs_1_), channel_id=1, source_target_pairs={{0,32},{1,33},{2,34},{3,35},{4,36},{5,37},{6,38},{7,39},{8,40},{9,... | collective-permute-start | bytes 393224 | tf_op jit(solution)/shard_map/ppermute | solution.py:269
  95.3 27.0 %all-to-all-done.1.parts_ref = bf16[32,10,128]{2,1,0:T(8,128)(2,1)S(1)} async-done(((bf16[32,10,128]{2,1,0:T(8,128)(2,1)}), bf16[32,10,128]{2,1,0:T(8,128)(2,1)S(1)}, u32[]{:S(2)}, u32[]{:S(2)}) %all-to-all-start.1) | async-done | bytes 81952 | tf_op jit(solution)/shard_map/all_to_all | solution.py:273
  122.4 0.0 copy-start.6
  122.4 0.7 copy-done.6
  123.0 1.6 %chip_sum.1 = bf16[16,10,128]{2,1,0:T(8,128)(2,1)} custom-call(bf16[32,10,128]{2,1,0:T(8,128)(2,1)} %copy-done.6), custom_call_target="tpu_custom_call" | custom-call | tf_op jit(solution)/shard_map/chip_sum/pallas_call | solution.py:218
  124.6 3.6 %all-to-all-start.2 = ((bf16[16,10,128]{2,1,0:T(8,128)(2,1)}), bf16[16,10,128]{2,1,0:T(8,128)(2,1)S(1)}, u32[]{:S(2)}, u32[]{:S(2)}) async-start(bf16[16,10,128]{2,1,0:T(8,128)(2,1)} %chip_sum.1), calls=%async_computation.2 | async-start | bytes 131072 | tf_op jit(solution)/shard_map/all_to_all | solution.py:276
  128.2 0.0 collective-permute-done.refs_2_
  128.2 0.0 copy-start.8
  128.2 7.6 %all-to-all-done.2.refs_3_ = bf16[16,10,128]{2,1,0:T(8,128)(2,1)S(1)} async-done(((bf16[16,10,128]{2,1,0:T(8,128)(2,1)}), bf16[16,10,128]{2,1,0:T(8,128)(2,1)S(1)}, u32[]{:S(2)}, u32[]{:S(2)}) %all-to-all-start.2) | async-done | bytes 40992 | tf_op jit(solution)/shard_map/all_to_all | solution.py:276
  135.8 0.0 copy-start.7
  135.8 0.0 copy-done.8
  135.8 0.6 copy-done.7
  136.4 1.7 %finish.1 = (bf16[1,128,512]{2,1,0:T(8,128)(2,1)}, f32[8,2048]{1,0:T(8,128)}, f32[8,512]{1,0:T(8,128)}) custom-call(s32[32]{0:T(128)} %bitcast.3, bf16[1,128,512]{2,1,0:T(8,128)(2,1)} %copy-done.4, bf16[1,128,512]{2,1,0:T(8,128)(2,1)} %copy-done.8, bf16[16,10,128]{2,1,0:T(8,128)(2,1)} %copy-done.7), custom_call_target="tpu_custom_call" | custom-call | tf_op jit(solution)/shard_map/finish/pallas_call | solution.py:249
Async XLA Ops:
  0.6 1.6 %copy-start = (bf16[512,2048]{1,0:T(8,128)(2,1)S(1)}, bf16[512,2048]{1,0:T(8,128)(2,1)}, u32[]{:S(2)}) copy-start(bf16[512,2048]{1,0:T(8,128)(2,1)} %win_ref.1) | copy-start | bytes 6291460
  2.2 1.0 copy-start.1
  3.3 0.9 copy-start.2
  4.2 0.9 copy-start.3
  5.1 0.7 copy-start.5
  11.2 63.3 %copy-start.4 = (bf16[1,128,512]{2,1,0:T(8,128)(2,1)}, bf16[1,128,512]{2,1,0:T(8,128)(2,1)S(1)}, u32[]{:S(2)}) copy-start(bf16[1,128,512]{2,1,0:T(8,128)(2,1)S(1)} %get-tuple-element.11.refs_1_) | copy-start | bytes 393220
  11.2 4.9 %collective-permute-start.1 = (bf16[16,320,128]{2,1,0:T(8,128)(2,1)S(1)}, bf16[16,320,128]{2,1,0:T(8,128)(2,1)S(1)}, u32[]{:S(2)}, u32[]{:S(2)}) collective-permute-start(bf16[16,320,128]{2,1,0:T(8,128)(2,1)S(1)} %get-tuple-element.13), channel_id=1, source_target_pairs={{0,1},{1,0},{2,3},{3,2},{4,5},{5,4},{6,7},{7,6},{8,9},{9,8},{10,11... | collective-permute-start | bytes 3932168 | tf_op jit(solution)/shard_map/ppermute | solution.py:268
  45.9 76.5 %all-to-all-start.1 = ((bf16[32,10,128]{2,1,0:T(8,128)(2,1)}), bf16[32,10,128]{2,1,0:T(8,128)(2,1)S(1)}, u32[]{:S(2)}, u32[]{:S(2)}) async-start(bf16[32,10,128]{2,1,0:T(8,128)(2,1)} %group_sum.1), calls=%async_computation.1 | async-start | bytes 262144 | tf_op jit(solution)/shard_map/all_to_all | solution.py:273
  74.5 53.6 %collective-permute-start = (bf16[1,128,512]{2,1,0:T(8,128)(2,1)S(1)}, bf16[1,128,512]{2,1,0:T(8,128)(2,1)S(1)}, u32[]{:S(2)}, u32[]{:S(2)}) collective-permute-start(bf16[1,128,512]{2,1,0:T(8,128)(2,1)S(1)} %get-tuple-element.11.refs_1_), channel_id=1, source_target_pairs={{0,32},{1,33},{2,34},{3,35},{4,36},{5,37},{6,38},{7,39},{8,40},{9,... | collective-permute-start | bytes 393224 | tf_op jit(solution)/shard_map/ppermute | solution.py:269
  122.4 0.7 copy-start.6
  124.6 11.2 %all-to-all-start.2 = ((bf16[16,10,128]{2,1,0:T(8,128)(2,1)}), bf16[16,10,128]{2,1,0:T(8,128)(2,1)S(1)}, u32[]{:S(2)}, u32[]{:S(2)}) async-start(bf16[16,10,128]{2,1,0:T(8,128)(2,1)} %chip_sum.1), calls=%async_computation.2 | async-start | bytes 131072 | tf_op jit(solution)/shard_map/all_to_all | solution.py:276
  128.2 7.7 %copy-start.8 = (bf16[1,128,512]{2,1,0:T(8,128)(2,1)}, bf16[1,128,512]{2,1,0:T(8,128)(2,1)S(1)}, u32[]{:S(2)}) copy-start(bf16[1,128,512]{2,1,0:T(8,128)(2,1)S(1)} %collective-permute-done.refs_2_) | copy-start | bytes 393220
  135.8 0.6 copy-start.7

commit v2 on v1

--- a/solution.py
+++ b/solution.py
@@ -6,6 +6,7 @@
 from jax.experimental import pallas as pl
 from jax.experimental.pallas import tpu as pltpu
 from jax.sharding import PartitionSpec as P
+
 
 HEADS = 8
 HEAD_DIM = 64
@@ -15,6 +16,7 @@
 CHIPS = 32
 CORES = 2
 ROWS = 320
+PIECE = 10
 epsilon = 1e-06
 f32 = jnp.float32
 bf16 = jnp.bfloat16
@@ -37,11 +39,11 @@
 
 
 def layer_kernel(
-    lengths_ref,
-    x_ref,
-    up_ref,
-    win_ref,
-    wout_ref,
+    lengths_hbm,
+    x_hbm,
+    up_hbm,
+    win_hbm,
+    wout_hbm,
     home_ref,
     xgrad_ref,
     send_ref,
@@ -53,23 +55,40 @@
     hgrad_ref,
     normed_t,
     gated_t,
+    lengths_ref,
+    x_ref,
+    up_ref,
+    win_ref,
+    wout_ref,
+    arrivals,
 ):
+    parts = [(x_hbm.at[0], x_ref)]
+    parts += [(win_hbm.at[:, pl.ds(j * D, D)], win_ref.at[:, pl.ds(j * D, D)]) for j in range(4)]
+    parts += [(lengths_hbm, lengths_ref), (wout_hbm, wout_ref), (up_hbm.at[0], up_ref)]
+    copies = [
+        pltpu.make_async_copy(src, dst, arrivals.at[i]) for i, (src, dst) in enumerate(parts)
+    ]
+    for copy in copies:
+        copy.start()
     position = lax.axis_index("wide")
-    length = lengths_ref[position]
     core = lax.rem(position, 2)
-    x = x_ref[0].astype(f32)
+    copies[0].wait()
+    x = x_ref[...].astype(f32)
     inverse = lax.rsqrt(jnp.mean(x * x, axis=-1, keepdims=True) + epsilon)
     unit = x * inverse
     normed = unit.astype(bf16)
     normed_t[...] = unit.astype(bf16).astype(f32).T.reshape(CHIPS, 16, LEN)
     for part in range(4):
         columns = pl.ds(part * D, D)
+        copies[1 + part].wait()
         hidden = nn(normed, win_ref[:, columns])
         sig = sigmoid(hidden)
         activated = hidden * sig
         act_ref[:, columns] = activated.astype(bf16)
         slope_ref[:, columns] = sig + activated * (1.0 - sig)
 
+    copies[5].wait()
+    length = lengths_ref[position]
     query_at = lax.broadcasted_iota(jnp.int32, (LEN, LEN), 0)
     key_at = lax.broadcasted_iota(jnp.int32, (LEN, LEN), 1)
     allowed = (key_at <= query_at) & (key_at < length)
@@ -106,10 +125,12 @@
     gate = act_ref[:, :D].astype(f32)
     gated = (gate * unit_attended).astype(bf16)
     gated_t[...] = gated.astype(f32).T
+    copies[6].wait()
     home_ref[0] = (x + nn(gated, wout_ref[...])).astype(bf16)
 
+    copies[7].wait()
     alive = lax.broadcasted_iota(jnp.int32, (LEN, D), 0) < length
-    masked_wide = jnp.where(alive, up_ref[0].astype(f32), 0.0)
+    masked_wide = jnp.where(alive, up_ref[...].astype(f32), 0.0)
     masked = masked_wide.astype(bf16)
     gated_grad = nt(masked, wout_ref[...]).astype(bf16).astype(f32)
     hgrad_ref[:, :D] = (
@@ -158,15 +179,19 @@
                 ]
 
 
+def kept_in(space, *arrays):
+    return [pltpu.with_memory_space_constraint(array, space) for array in arrays]
+
+
 def layer(lengths, x, up, win, wout):
     vmem = pl.BlockSpec(memory_space=pltpu.VMEM)
-    smem = pl.BlockSpec(memory_space=pltpu.SMEM)
+    hbm = pl.BlockSpec(memory_space=pltpu.HBM)
     block = jax.ShapeDtypeStruct((1, LEN, D), bf16)
     grads = jax.ShapeDtypeStruct((GROUPS, ROWS, 128), bf16)
     return pl.pallas_call(
         layer_kernel,
         out_shape=(block, block, grads, grads),
-        in_specs=[smem, vmem, vmem, vmem, vmem],
+        in_specs=[hbm] * 5,
         out_specs=(vmem, vmem, vmem, vmem),
         scratch_shapes=[
             pltpu.VMEM((LEN, 4 * D), bf16),
@@ -176,55 +201,69 @@
             pltpu.VMEM((LEN, 4 * D), bf16),
             pltpu.VMEM((CHIPS, 16, LEN), f32),
             pltpu.VMEM((D, LEN), f32),
+            pltpu.SMEM((2 * CHIPS,), jnp.int32),
+            pltpu.VMEM((LEN, D), bf16),
+            pltpu.VMEM((LEN, D), bf16),
+            pltpu.VMEM((D, 4 * D), bf16),
+            pltpu.VMEM((D, D), bf16),
+            pltpu.SemaphoreType.DMA((8,)),
         ],
         compiler_params=pltpu.CompilerParams(vmem_limit_bytes=40 << 20),
         name="layer",
-    )(lengths, x, up, win, wout)
-
-
-def group_sum_kernel(parts_ref, out_ref, total):
+    )(*kept_in(pltpu.HBM, lengths, x, up, win, wout))
+
+
+def group_sum_kernel(parts_ref, out_ref, total, ordered):
     summed = parts_ref[0].astype(f32)
     for g in range(1, GROUPS):
         summed += parts_ref[g].astype(f32)
     total[...] = summed
     for z in range(CHIPS):
-        out_ref[z, 0:8, :] = total[8 * z : 8 * z + 8, :].astype(bf16)
-        out_ref[z, 8:10, :] = total[pl.ds(256 + z, 2, stride=CHIPS), :].astype(bf16)
+        ordered[PIECE * z : PIECE * z + 8, :] = total[8 * z : 8 * z + 8, :]
+        ordered[PIECE * z + 8 : PIECE * z + 10, :] = total[pl.ds(256 + z, 2, stride=CHIPS), :]
+    out_ref[...] = ordered[...].astype(bf16)
 
 
 def group_sum(parts):
     vmem = pl.BlockSpec(memory_space=pltpu.VMEM)
     return pl.pallas_call(
         group_sum_kernel,
-        out_shape=jax.ShapeDtypeStruct((CHIPS, 10, 128), bf16),
+        out_shape=jax.ShapeDtypeStruct((CHIPS * PIECE, 128), bf16),
         in_specs=[vmem],
         out_specs=vmem,
-        scratch_shapes=[pltpu.VMEM((ROWS, 128), f32)],
+        scratch_shapes=[pltpu.VMEM((ROWS, 128), f32), pltpu.VMEM((CHIPS * PIECE, 128), f32)],
         name="group_sum",
-    )(parts)
-
-
-def chip_sum_kernel(parts_ref, out_ref):
-    summed = parts_ref[0].astype(f32)
+    )(*kept_in(pltpu.VMEM, parts))
+
+
+def chip_sum_kernel(parts_ref, out_ref, parts, copies):
+    parts[...] = parts_ref[...].astype(f32)
+    summed = parts[0:PIECE, :]
     for z in range(1, CHIPS):
-        summed += parts_ref[z].astype(f32)
-    summed = summed.astype(bf16)
+        summed += parts[PIECE * z : PIECE * (z + 1), :]
     for g in range(GROUPS):
-        out_ref[g] = summed
+        copies[PIECE * g : PIECE * (g + 1), :] = summed
+    out_ref[...] = copies[...].astype(bf16)
 
 
 def chip_sum(parts):
     vmem = pl.BlockSpec(memory_space=pltpu.VMEM)
     return pl.pallas_call(
         chip_sum_kernel,
-        out_shape=jax.ShapeDtypeStruct((GROUPS, 10, 128), bf16),
+        out_shape=jax.ShapeDtypeStruct((GROUPS * PIECE, 128), bf16),
         in_specs=[vmem],
         out_specs=vmem,
+        scratch_shapes=[
+            pltpu.VMEM((CHIPS * PIECE, 128), f32),
+            pltpu.VMEM((GROUPS * PIECE, 128), f32),
+        ],
         name="chip_sum",
-    )(parts)
-
-
-def finish_kernel(scale, swap_ref, home_ref, arrived_ref, parts_ref, out_ref, din_ref, dout_ref):
+    )(*kept_in(pltpu.VMEM, parts))
+
+
+def finish_kernel(
+    scale, swap_ref, home_ref, arrived_ref, parts_ref, out_ref, din_ref, dout_ref, parts
+):
     position = lax.axis_index("wide")
     chosen = swap_ref[lax.rem(position, CHIPS)] == 1
 
@@ -236,11 +275,13 @@
     def _():
         out_ref[...] = home_ref[...]
 
+    parts[...] = parts_ref[...].astype(f32) * scale
     for g in range(GROUPS):
-        piece = parts_ref[g].astype(f32) * scale
-        din_ref[:, g * 128 : (g + 1) * 128] = piece[:8]
+        din_ref[:, g * 128 : (g + 1) * 128] = parts[PIECE * g : PIECE * g + 8, :]
         block, pair = g // 4, g % 4
-        dout_ref[2 * pair : 2 * pair + 2, block * 128 : (block + 1) * 128] = piece[8:10]
+        dout_ref[2 * pair : 2 * pair + 2, block * 128 : (block + 1) * 128] = parts[
+            PIECE * g + 8 : PIECE * g + 10, :
+        ]
 
 
 def finish(scale, swaps, home, arrived, parts):
@@ -255,8 +296,15 @@
         ),
         in_specs=[smem, vmem, vmem, vmem],
         out_specs=(vmem, vmem, vmem),
+        scratch_shapes=[pltpu.VMEM((GROUPS * PIECE, 128), f32)],
         name="finish",
-    )(swaps, home, arrived, parts)
+    )(swaps, *kept_in(pltpu.VMEM, home, arrived, parts))
+
+
+def exchanged(rows, count, axis, groups=None):
+    pieces = rows.reshape(count, PIECE // 2, 2, 128)
+    pieces = lax.all_to_all(pieces, axis, 0, 0, tiled=True, axis_index_groups=groups)
+    return pieces.reshape(count * PIECE, 128)
 
 
 def body(sequences, upstream, lengths, swap_table, input_weight, output_weight):
@@ -270,10 +318,9 @@
     chip = (keep.astype(f32) + received.astype(f32)).astype(bf16)
     parts = lax.all_to_all(chip, "grp", 0, 0, tiled=True)
     same_core = [[2 * z + c for z in range(CHIPS)] for c in range(CORES)]
-    parts = lax.all_to_all(
-        group_sum(parts), "wide", 0, 0, tiled=True, axis_index_groups=same_core
-    )
-    parts = lax.all_to_all(chip_sum(parts), "grp", 0, 0, tiled=True)
+    parts = group_sum(parts)
+    parts = exchanged(parts, CHIPS, "wide", same_core)
+    parts = exchanged(chip_sum(parts), GROUPS, "grp")
     scale = 1.0 / math.sqrt(LEN * wide * lax.axis_size("grp"))
     layer_out, total_in, total_out = finish(
         scale, swap_table.reshape(half), home, arrived, parts

time: 139 us -> 128 us (0.921)
  the two profiles are of different devices: /device:TPU:32 before, /device:TPU:2 now
where the time goes in v2:
time: 128 us
  starting transfers between devices  49.1 us (38%)
  blocking collectives  34.9 us (27%)
  waiting for transfers between devices  33 us (26%)
  Pallas kernels  9.52 us (7%)
    all_to_all x1, blocking collectives, body(): parts = lax.all_to_all(chip, 'grp', 0, 0, tiled=True)  34.9 us
    all_to_all x2, waiting for transfers between devices, exchanged(): lax.all_to_all(pieces, axis, 0, 0, tiled=True, axis_index_groups=groups)  30 us
    all_to_all x2, starting transfers between devices, exchanged(): lax.all_to_all(pieces, axis, 0, 0, tiled=True, axis_index_groups=groups)  25.1 us
    ppermute x1, starting transfers between devices, body(): lax.ppermute(home, 'wide', [(i, (i + half) % wide) for i in range(wide)])  22 us
    pallas_call x1, Pallas kernels, layer(): pl.pallas_call(layer_kernel, out_shape=(block, block, grads, grads), in_s...  6.62 us
    ppermute x1, waiting for transfers between devices, body(): received = lax.ppermute(send, 'wide', [(i, i ^ 1) for i in range(wide)])  3 us
  transfers between devices with their start and end apart: 4, of which 3 were waited for; matrix products, arithmetic and copies ran while one was open for 0% of the time, Pallas kernels for 1%

profile of v2, /device:TPU:2, one launch (start us, length us, event | category | flops | bytes accessed | tf_op | source)
XLA Modules:
  0.0 127.5 jit_solution(15077261302471339592)
XLA Ops:
  0.6 6.6 %layer.1 = (bf16[1,128,512]{2,1,0:T(8,128)(2,1)S(1)}, bf16[1,128,512]{2,1,0:T(8,128)(2,1)}, bf16[16,320,128]{2,1,0:T(8,128)(2,1)S(1)}, bf16[16,320,128]{2,1,0:T(8,128)(2,1)S(1)}) custom-call(s32[64]{0:T(128)} %bitcast.10, bf16[1,128,512]{2,1,0:T(8,128)(2,1)} %x_hbm.1, bf16[1,128,512]{2,1,0:T(8,128)(2,1)} %up_hbm.1, bf16[512,2048]{1,0:T(8,128)(2,1)} %win_hbm.1, ...), custom_call_target="tpu_custom_call" | custom-call | tf_op jit(solution)/shard_map/layer/pallas_call | solution.py:191
  7.3 1.9 %collective-permute-start.1 = (bf16[16,320,128]{2,1,0:T(8,128)(2,1)S(1)}, bf16[16,320,128]{2,1,0:T(8,128)(2,1)S(1)}, u32[]{:S(2)}, u32[]{:S(2)}) collective-permute-start(bf16[16,320,128]{2,1,0:T(8,128)(2,1)S(1)} %get-tuple-element.13), channel_id=1, source_target_pairs={{0,1},{1,0},{2,3},{3,2},{4,5},{5,4},{6,7},{7,6},{8,9},{9,8},{10,11... | collective-permute-start | bytes 3932168 | tf_op jit(solution)/shard_map/ppermute | solution.py:316
  9.2 3.0 %collective-permute-done.1 = bf16[16,320,128]{2,1,0:T(8,128)(2,1)S(1)} collective-permute-done((bf16[16,320,128]{2,1,0:T(8,128)(2,1)S(1)}, bf16[16,320,128]{2,1,0:T(8,128)(2,1)S(1)}, u32[]{:S(2)}, u32[]{:S(2)}) %collective-permute-start.1) | collective-permute-done | bytes 1310752 | tf_op jit(solution)/shard_map/ppermute | solution.py:316
  12.2 0.3 add_convert_fusion
  12.5 34.9 %all_to_all.15.parts_ref = bf16[16,320,128]{2,1,0:T(8,128)(2,1)S(1)} all-to-all(bf16[16,320,128]{2,1,0:T(8,128)(2,1)S(1)} %add_convert_fusion), channel_id=1, replica_groups=mesh['grp'=16,'wide'=64] {'grp'}, dimensions={0} | all-to-all | bytes 2621440 | tf_op jit(solution)/shard_map/all_to_all | solution.py:319
  47.4 0.9 group_sum.1
  48.3 20.0 %all-to-all-start.1 = ((bf16[32,5,2,128]{3,2,1,0:T(2,128)(2,1)}), bf16[32,5,2,128]{3,2,1,0:T(2,128)(2,1)S(1)}, u32[]{:S(2)}, u32[]{:S(2)}) async-start(bf16[32,5,2,128]{3,2,1,0:T(2,128)(2,1)} %bitcast.8), calls=%async_computation.1 | async-start | bytes 163840 | tf_op jit(solution)/shard_map/all_to_all | solution.py:306
  68.3 22.0 %collective-permute-start = (bf16[1,128,512]{2,1,0:T(8,128)(2,1)S(1)}, bf16[1,128,512]{2,1,0:T(8,128)(2,1)S(1)}, u32[]{:S(2)}, u32[]{:S(2)}) collective-permute-start(bf16[1,128,512]{2,1,0:T(8,128)(2,1)S(1)} %get-tuple-element.11.refs_1_), channel_id=1, source_target_pairs={{0,32},{1,33},{2,34},{3,35},{4,36},{5,37},{6,38},{7,39},{8,40},{9,... | collective-permute-start | bytes 393224 | tf_op jit(solution)/shard_map/ppermute | solution.py:317
  90.3 23.8 %all-to-all-done.1 = bf16[32,5,2,128]{3,2,1,0:T(2,128)(2,1)S(1)} async-done(((bf16[32,5,2,128]{3,2,1,0:T(2,128)(2,1)}), bf16[32,5,2,128]{3,2,1,0:T(2,128)(2,1)S(1)}, u32[]{:S(2)}, u32[]{:S(2)}) %all-to-all-start.1) | async-done | bytes 81952 | tf_op jit(solution)/shard_map/all_to_all | solution.py:306
  114.1 0.7 chip_sum.1
  114.8 5.1 %all-to-all-start.2 = ((bf16[16,5,2,128]{3,2,1,0:T(2,128)(2,1)}), bf16[16,5,2,128]{3,2,1,0:T(2,128)(2,1)S(1)}, u32[]{:S(2)}, u32[]{:S(2)}) async-start(bf16[16,5,2,128]{3,2,1,0:T(2,128)(2,1)} %bitcast.9), calls=%async_computation.2 | async-start | bytes 81920 | tf_op jit(solution)/shard_map/all_to_all | solution.py:306
  119.9 0.0 collective-permute-done.refs_2_
  119.9 6.2 %all-to-all-done.2 = bf16[16,5,2,128]{3,2,1,0:T(2,128)(2,1)S(1)} async-done(((bf16[16,5,2,128]{3,2,1,0:T(2,128)(2,1)}), bf16[16,5,2,128]{3,2,1,0:T(2,128)(2,1)S(1)}, u32[]{:S(2)}, u32[]{:S(2)}) %all-to-all-start.2) | async-done | bytes 40992 | tf_op jit(solution)/shard_map/all_to_all | solution.py:306
  126.2 1.4 %finish.1 = (bf16[1,128,512]{2,1,0:T(8,128)(2,1)}, f32[8,2048]{1,0:T(8,128)}, f32[8,512]{1,0:T(8,128)}) custom-call(s32[32]{0:T(128)} %bitcast.11, bf16[1,128,512]{2,1,0:T(8,128)(2,1)S(1)} %get-tuple-element.11.refs_1_, bf16[1,128,512]{2,1,0:T(8,128)(2,1)S(1)} %collective-permute-done.refs_2_, bf16[160,128]{1,0:T(8,128)(2,1)S(1)} %bitcast.7), custom_call_target="tpu_custom_call" | custom-call | tf_op jit(solution)/shard_map/finish/pallas_call | solution.py:290
Async XLA Ops:
  7.3 4.9 %collective-permute-start.1 = (bf16[16,320,128]{2,1,0:T(8,128)(2,1)S(1)}, bf16[16,320,128]{2,1,0:T(8,128)(2,1)S(1)}, u32[]{:S(2)}, u32[]{:S(2)}) collective-permute-start(bf16[16,320,128]{2,1,0:T(8,128)(2,1)S(1)} %get-tuple-element.13), channel_id=1, source_target_pairs={{0,1},{1,0},{2,3},{3,2},{4,5},{5,4},{6,7},{7,6},{8,9},{9,8},{10,11... | collective-permute-start | bytes 3932168 | tf_op jit(solution)/shard_map/ppermute | solution.py:316
  48.3 65.9 %all-to-all-start.1 = ((bf16[32,5,2,128]{3,2,1,0:T(2,128)(2,1)}), bf16[32,5,2,128]{3,2,1,0:T(2,128)(2,1)S(1)}, u32[]{:S(2)}, u32[]{:S(2)}) async-start(bf16[32,5,2,128]{3,2,1,0:T(2,128)(2,1)} %bitcast.8), calls=%async_computation.1 | async-start | bytes 163840 | tf_op jit(solution)/shard_map/all_to_all | solution.py:306
  68.3 51.6 %collective-permute-start = (bf16[1,128,512]{2,1,0:T(8,128)(2,1)S(1)}, bf16[1,128,512]{2,1,0:T(8,128)(2,1)S(1)}, u32[]{:S(2)}, u32[]{:S(2)}) collective-permute-start(bf16[1,128,512]{2,1,0:T(8,128)(2,1)S(1)} %get-tuple-element.11.refs_1_), channel_id=1, source_target_pairs={{0,32},{1,33},{2,34},{3,35},{4,36},{5,37},{6,38},{7,39},{8,40},{9,... | collective-permute-start | bytes 393224 | tf_op jit(solution)/shard_map/ppermute | solution.py:317
  114.8 11.3 %all-to-all-start.2 = ((bf16[16,5,2,128]{3,2,1,0:T(2,128)(2,1)}), bf16[16,5,2,128]{3,2,1,0:T(2,128)(2,1)S(1)}, u32[]{:S(2)}, u32[]{:S(2)}) async-start(bf16[16,5,2,128]{3,2,1,0:T(2,128)(2,1)} %bitcast.9), calls=%async_computation.2 | async-start | bytes 81920 | tf_op jit(solution)/shard_map/all_to_all | solution.py:306

commit v3 on v2

--- a/solution.py
+++ b/solution.py
@@ -38,6 +38,19 @@
     return 0.5 * jnp.tanh(0.5 * x) + 0.5
 
 
+def store_grads(out_ref, mine_in, mine_out, hgrad_ref, masked):
+    for block in range(4):
+        grads = nn(mine_in, hgrad_ref[:, block * 512 : (block + 1) * 512]).astype(bf16)
+        for j in range(4):
+            out_ref[4 * block + j, 0:256, :] = grads[:, j * 128 : (j + 1) * 128]
+    grads = nn(mine_out, masked).astype(bf16)
+    for block in range(4):
+        for p in range(4):
+            out_ref[4 * block + p, 256:320, :] = grads[
+                p * 64 : (p + 1) * 64, block * 128 : (block + 1) * 128
+            ]
+
+
 def layer_kernel(
     lengths_hbm,
     x_hbm,
@@ -45,14 +58,15 @@
     win_hbm,
     wout_hbm,
     home_ref,
-    xgrad_ref,
     send_ref,
-    keep_ref,
+    hgrad_ref,
+    masked_ref,
+    keep_in_ref,
+    keep_out_ref,
     act_ref,
     slope_ref,
     wslope_ref,
     weights_ref,
-    hgrad_ref,
     normed_t,
     gated_t,
     lengths_ref,
@@ -130,8 +144,8 @@
 
     copies[7].wait()
     alive = lax.broadcasted_iota(jnp.int32, (LEN, D), 0) < length
-    masked_wide = jnp.where(alive, up_ref[...].astype(f32), 0.0)
-    masked = masked_wide.astype(bf16)
+    masked = jnp.where(alive, up_ref[...].astype(f32), 0.0).astype(bf16)
+    masked_ref[...] = masked
     gated_grad = nt(masked, wout_ref[...]).astype(bf16).astype(f32)
     hgrad_ref[:, :D] = (
         (gated_grad * unit_attended).astype(bf16).astype(f32) * slope_ref[:, :D]
@@ -158,25 +172,39 @@
             columns = pl.ds(start + at, 128)
             hgrad_ref[:, columns] = (grad * slope_ref[:, columns]).astype(bf16)
 
+    def mine(side):
+        rows = pl.ds(pl.multiple_of(side * 8, 8), 8)
+        mine_in = normed_t[:, rows, :].reshape(256, LEN).astype(bf16)
+        mine_out = jnp.concatenate(
+            [gated_t[pl.ds(side * 8 + i, CHIPS, stride=16), :] for i in range(8)], axis=0
+        ).astype(bf16)
+        return mine_in, mine_out
+
+    keep_in_ref[...], keep_out_ref[...] = mine(core)
+    store_grads(send_ref, *mine(1 - core), hgrad_ref, masked)
+
+
+def keep_kernel(keep_in_ref, keep_out_ref, hgrad_ref, masked_ref, keep_ref):
+    store_grads(keep_ref, keep_in_ref[...], keep_out_ref[...], hgrad_ref, masked_ref[...])
+
+
+def input_grad_kernel(x_hbm, win_hbm, hgrad_ref, masked_ref, xgrad_ref, x_ref, win_ref, arrivals):
+    copies = [
+        pltpu.make_async_copy(x_hbm.at[0], x_ref, arrivals.at[0]),
+        pltpu.make_async_copy(win_hbm, win_ref, arrivals.at[1]),
+    ]
+    for copy in copies:
+        copy.start()
+    copies[0].wait()
+    x = x_ref[...].astype(f32)
+    inverse = lax.rsqrt(jnp.mean(x * x, axis=-1, keepdims=True) + epsilon)
+    unit = x * inverse
+    copies[1].wait()
     unit_grad = nt(hgrad_ref[...], win_ref[...])
     overlap = jnp.mean(unit_grad * unit, axis=-1, keepdims=True)
-    xgrad_ref[0] = (masked_wide + inverse * (unit_grad - unit * overlap)).astype(bf16)
-
-    for out_ref, side in ((send_ref, 1 - core), (keep_ref, core)):
-        mine = normed_t[:, pl.ds(pl.multiple_of(side * 8, 8), 8), :].reshape(256, LEN).astype(bf16)
-        for block in range(4):
-            grads = nn(mine, hgrad_ref[:, block * 512 : (block + 1) * 512]).astype(bf16)
-            for j in range(4):
-                out_ref[4 * block + j, 0:256, :] = grads[:, j * 128 : (j + 1) * 128]
-        mine = jnp.concatenate(
-            [gated_t[pl.ds(side * 8 + i, CHIPS, stride=16), :] for i in range(8)], axis=0
-        ).astype(bf16)
-        grads = nn(mine, masked).astype(bf16)
-        for block in range(4):
-            for p in range(4):
-                out_ref[4 * block + p, 256:320, :] = grads[
-                    p * 64 : (p + 1) * 64, block * 128 : (block + 1) * 128
-                ]
+    xgrad_ref[0] = (
+        masked_ref[...].astype(f32) + inverse * (unit_grad - unit * overlap)
+    ).astype(bf16)
 
 
 def kept_in(space, *arrays):
@@ -186,19 +214,24 @@
 def layer(lengths, x, up, win, wout):
     vmem = pl.BlockSpec(memory_space=pltpu.VMEM)
     hbm = pl.BlockSpec(memory_space=pltpu.HBM)
-    block = jax.ShapeDtypeStruct((1, LEN, D), bf16)
-    grads = jax.ShapeDtypeStruct((GROUPS, ROWS, 128), bf16)
+    shapes = [
+        (1, LEN, D),
+        (GROUPS, ROWS, 128),
+        (LEN, 4 * D),
+        (LEN, D),
+        (256, LEN),
+        (256, LEN),
+    ]
     return pl.pallas_call(
         layer_kernel,
-        out_shape=(block, block, grads, grads),
+        out_shape=[jax.ShapeDtypeStruct(shape, bf16) for shape in shapes],
         in_specs=[hbm] * 5,
-        out_specs=(vmem, vmem, vmem, vmem),
+        out_specs=[vmem] * 6,
         scratch_shapes=[
             pltpu.VMEM((LEN, 4 * D), bf16),
             pltpu.VMEM((LEN, 4 * D), f32),
             pltpu.VMEM((HEADS, LEN, LEN), f32),
             pltpu.VMEM((HEADS // 2, 2 * LEN, LEN), bf16),
-            pltpu.VMEM((LEN, 4 * D), bf16),
             pltpu.VMEM((CHIPS, 16, LEN), f32),
             pltpu.VMEM((D, LEN), f32),
             pltpu.SMEM((2 * CHIPS,), jnp.int32),
@@ -208,9 +241,56 @@
             pltpu.VMEM((D, D), bf16),
             pltpu.SemaphoreType.DMA((8,)),
         ],
-        compiler_params=pltpu.CompilerParams(vmem_limit_bytes=40 << 20),
+        compiler_params=pltpu.CompilerParams(vmem_limit_bytes=24 << 20),
         name="layer",
     )(*kept_in(pltpu.HBM, lengths, x, up, win, wout))
+
+
+def kept_half(keep_in, keep_out, hgrad, masked):
+    vmem = pl.BlockSpec(memory_space=pltpu.VMEM)
+    return pl.pallas_call(
+        keep_kernel,
+        out_shape=jax.ShapeDtypeStruct((GROUPS, ROWS, 128), bf16),
+        in_specs=[vmem] * 4,
+        out_specs=vmem,
+        compiler_params=pltpu.CompilerParams(vmem_limit_bytes=8 << 20),
+        name="kept_half",
+    )(*kept_in(pltpu.VMEM, keep_in, keep_out, hgrad, masked))
+
+
+def input_gradient(x, win, hgrad, masked):
+    vmem = pl.BlockSpec(memory_space=pltpu.VMEM)
+    hbm = pl.BlockSpec(memory_space=pltpu.HBM)
+    return pl.pallas_call(
+        input_grad_kernel,
+        out_shape=jax.ShapeDtypeStruct((1, LEN, D), bf16),
+        in_specs=[hbm, hbm, vmem, vmem],
+        out_specs=vmem,
+        scratch_shapes=[
+            pltpu.VMEM((LEN, D), bf16),
+            pltpu.VMEM((D, 4 * D), bf16),
+            pltpu.SemaphoreType.DMA((2,)),
+        ],
+        compiler_params=pltpu.CompilerParams(vmem_limit_bytes=8 << 20),
+        name="input_gradient",
+    )(*kept_in(pltpu.HBM, x, win), *kept_in(pltpu.VMEM, hgrad, masked))
+
+
+def chip_half_kernel(keep_ref, received_ref, out_ref):
+    for g in range(GROUPS):
+        out_ref[g] = (keep_ref[g].astype(f32) + received_ref[g].astype(f32)).astype(bf16)
+
+
+def chip_half(keep, received):
+    vmem = pl.BlockSpec(memory_space=pltpu.VMEM)
+    return pl.pallas_call(
+        chip_half_kernel,
+        out_shape=jax.ShapeDtypeStruct((GROUPS, ROWS, 128), bf16),
+        in_specs=[vmem, vmem],
+        out_specs=vmem,
+        compiler_params=pltpu.CompilerParams(vmem_limit_bytes=8 << 20),
+        name="chip_half",
+    )(*kept_in(pltpu.VMEM, keep, received))
 
 
 def group_sum_kernel(parts_ref, out_ref, total, ordered):
@@ -232,6 +312,7 @@
         in_specs=[vmem],
         out_specs=vmem,
         scratch_shapes=[pltpu.VMEM((ROWS, 128), f32), pltpu.VMEM((CHIPS * PIECE, 128), f32)],
+        compiler_params=pltpu.CompilerParams(vmem_limit_bytes=8 << 20),
         name="group_sum",
     )(*kept_in(pltpu.VMEM, parts))
 
@@ -257,19 +338,34 @@
             pltpu.VMEM((CHIPS * PIECE, 128), f32),
             pltpu.VMEM((GROUPS * PIECE, 128), f32),
         ],
+        compiler_params=pltpu.CompilerParams(vmem_limit_bytes=8 << 20),
         name="chip_sum",
     )(*kept_in(pltpu.VMEM, parts))
 
 
 def finish_kernel(
-    scale, swap_ref, home_ref, arrived_ref, parts_ref, out_ref, din_ref, dout_ref, parts
+    scale,
+    swap_ref,
+    home_ref,
+    to_early_ref,
+    to_late_ref,
+    parts_ref,
+    out_ref,
+    din_ref,
+    dout_ref,
+    parts,
 ):
     position = lax.axis_index("wide")
     chosen = swap_ref[lax.rem(position, CHIPS)] == 1
-
-    @pl.when(chosen)
+    late = (position >= CHIPS // 2) & (position < CHIPS * 3 // 2)
+
+    @pl.when(chosen & late)
     def _():
-        out_ref[...] = arrived_ref[...]
+        out_ref[...] = to_late_ref[...]
+
+    @pl.when(chosen & jnp.logical_not(late))
+    def _():
+        out_ref[...] = to_early_ref[...]
 
     @pl.when(jnp.logical_not(chosen))
     def _():
@@ -284,7 +380,7 @@
         ]
 
 
-def finish(scale, swaps, home, arrived, parts):
+def finish(scale, swaps, home, to_early, to_late, parts):
     vmem = pl.BlockSpec(memory_space=pltpu.VMEM)
     smem = pl.BlockSpec(memory_space=pltpu.SMEM)
     return pl.pallas_call(
@@ -294,11 +390,12 @@
             jax.ShapeDtypeStruct((8, 4 * D), f32),
             jax.ShapeDtypeStruct((8, D), f32),
         ),
-        in_specs=[smem, vmem, vmem, vmem],
+        in_specs=[smem, vmem, vmem, vmem, vmem],
         out_specs=(vmem, vmem, vmem),
         scratch_shapes=[pltpu.VMEM((GROUPS * PIECE, 128), f32)],
+        compiler_params=pltpu.CompilerParams(vmem_limit_bytes=8 << 20),
         name="finish",
-    )(swaps, *kept_in(pltpu.VMEM, home, arrived, parts))
+    )(swaps, *kept_in(pltpu.VMEM, home, to_early, to_late, parts))
 
 
 def exchanged(rows, count, axis, groups=None):
@@ -310,20 +407,25 @@
 def body(sequences, upstream, lengths, swap_table, input_weight, output_weight):
     wide = lax.axis_size("wide")
     half = wide // 2
-    home, input_grad, send, keep = layer(
+    home, send, hgrad, masked, keep_in, keep_out = layer(
         lengths.reshape(wide), sequences, upstream, input_weight, output_weight
     )
+    late = range(half // 2, half * 3 // 2)
+    route = [(i, (i + half) % wide) for i in range(wide)]
     received = lax.ppermute(send, "wide", [(i, i ^ 1) for i in range(wide)])
-    arrived = lax.ppermute(home, "wide", [(i, (i + half) % wide) for i in range(wide)])
-    chip = (keep.astype(f32) + received.astype(f32)).astype(bf16)
+    keep = kept_half(keep_in, keep_out, hgrad, masked)
+    to_early = lax.ppermute(home, "wide", [r for r in route if r[0] in late])
+    to_late = lax.ppermute(home, "wide", [r for r in route if r[1] in late])
+    chip = chip_half(keep, received)
     parts = lax.all_to_all(chip, "grp", 0, 0, tiled=True)
+    input_grad = input_gradient(sequences, input_weight, hgrad, masked)
+    parts = group_sum(parts)
     same_core = [[2 * z + c for z in range(CHIPS)] for c in range(CORES)]
-    parts = group_sum(parts)
     parts = exchanged(parts, CHIPS, "wide", same_core)
     parts = exchanged(chip_sum(parts), GROUPS, "grp")
     scale = 1.0 / math.sqrt(LEN * wide * lax.axis_size("grp"))
     layer_out, total_in, total_out = finish(
-        scale, swap_table.reshape(half), home, arrived, parts
+        scale, swap_table.reshape(half), home, to_early, to_late, parts
     )
     return (layer_out, input_grad, total_in, total_out)
 

time: 128 us -> 128 us (level)
  the two profiles are of different devices: /device:TPU:2 before, /device:TPU:64 now
where the time goes in v3:
time: 128 us
  starting transfers between devices  54.9 us (43%)
  waiting for transfers between devices  32.8 us (26%)
  blocking collectives  27.1 us (21%)
  Pallas kernels  12.5 us (10%)
    all_to_all x2, starting transfers between devices, exchanged(): lax.all_to_all(pieces, axis, 0, 0, tiled=True, axis_index_groups=groups)  31.7 us
    all_to_all x1, blocking collectives, body(): parts = lax.all_to_all(chip, 'grp', 0, 0, tiled=True)  27.1 us
    ppermute x1, waiting for transfers between devices, body(): to_early = lax.ppermute(home, 'wide', [r for r in route if r[0] in late])  21.9 us
    ppermute x1, starting transfers between devices, body(): to_late = lax.ppermute(home, 'wide', [r for r in route if r[1] in late])  19.9 us
    ppermute x1, waiting for transfers between devices, body(): to_late = lax.ppermute(home, 'wide', [r for r in route if r[1] in late])  6.41 us
    pallas_call x1, Pallas kernels, layer(): pl.pallas_call(layer_kernel, out_shape=[jax.ShapeDtypeStruct(shape, bf16)...  5.64 us
    pallas_call x1, Pallas kernels, input_gradient(): pl.pallas_call(input_grad_kernel, out_shape=jax.ShapeDtypeStruct((1, LEN,...  3.26 us
  transfers between devices with their start and end apart: 5, of which 4 were waited for; matrix products, arithmetic and copies ran while one was open for 0% of the time, Pallas kernels for 3%

profile of v3, /device:TPU:64, one launch (start us, length us, event | category | flops | bytes accessed | tf_op | source)
XLA Modules:
  0.0 127.9 jit_solution(2498703118397391642)
XLA Ops:
  0.6 5.6 %layer.1 = (bf16[1,128,512]{2,1,0:T(8,128)(2,1)S(1)}, bf16[16,320,128]{2,1,0:T(8,128)(2,1)S(1)}, bf16[128,2048]{1,0:T(8,128)(2,1)S(1)}, bf16[128,512]{1,0:T(8,12...) custom-call(s32[64]{0:T(128)} %bitcast.9, bf16[1,128,512]{2,1,0:T(8,128)(2,1)} %x_hbm.3, ...), custom_call_target="tpu_custom_call" | custom-call | tf_op jit(solution)/shard_map/layer/pallas_call | solution.py:225
  6.3 1.9 %collective-permute-start.2 = (bf16[16,320,128]{2,1,0:T(8,128)(2,1)S(1)}, bf16[16,320,128]{2,1,0:T(8,128)(2,1)S(1)}, u32[]{:S(2)}, u32[]{:S(2)}) collective-permute-start(bf16[16,320,128]{2,1,0:T(8,128)(2,1)S(1)} %get-tuple-element.18), channel_id=1, source_target_pairs={{0,1},{1,0},{2,3},{3,2},{4,5},{5,4},{6,7},{7,6},{8,9},{9,8},{10,11... | collective-permute-start | bytes 3932168 | tf_op jit(solution)/shard_map/ppermute | solution.py:415
  8.2 0.5 kept_half.1.keep_ref
  8.7 2.5 %collective-permute-done.2.received_ref = bf16[16,320,128]{2,1,0:T(8,128)(2,1)S(1)} collective-permute-done((bf16[16,320,128]{2,1,0:T(8,128)(2,1)S(1)}, bf16[16,320,128]{2,1,0:T(8,128)(2,1)S(1)}, u32[]{:S(2)}, u32[]{:S(2)}) %collective-permute-start.2) | collective-permute-done | bytes 1310752 | tf_op jit(solution)/shard_map/ppermute | solution.py:415
  11.2 0.3 chip_half.1
  11.5 27.1 %all_to_all.15.parts_ref = bf16[16,320,128]{2,1,0:T(8,128)(2,1)S(1)} all-to-all(bf16[16,320,128]{2,1,0:T(8,128)(2,1)S(1)} %chip_half.1), channel_id=1, replica_groups=mesh['grp'=16,'wide'=64] {'grp'}, dimensions={0} | all-to-all | bytes 2621440 | tf_op jit(solution)/shard_map/all_to_all | solution.py:420
  38.6 0.9 group_sum.1
  39.5 28.1 %all-to-all-start.1 = ((bf16[32,5,2,128]{3,2,1,0:T(2,128)(2,1)}), bf16[32,5,2,128]{3,2,1,0:T(2,128)(2,1)S(1)}, u32[]{:S(2)}, u32[]{:S(2)}) async-start(bf16[32,5,2,128]{3,2,1,0:T(2,128)(2,1)} %bitcast.2), calls=%async_computation.1 | async-start | bytes 163840 | tf_op jit(solution)/shard_map/all_to_all | solution.py:403
  67.6 19.9 %collective-permute-start.1 = (bf16[1,128,512]{2,1,0:T(8,128)(2,1)S(1)}, bf16[1,128,512]{2,1,0:T(8,128)(2,1)S(1)}, u32[]{:S(2)}, u32[]{:S(2)}) collective-permute-start(bf16[1,128,512]{2,1,0:T(8,128)(2,1)S(1)} %get-tuple-element.13.refs_1_), channel_id=1, source_target_pairs={{0,32},{1,33},{2,34},{3,35},{4,36},{5,37},{6,38},{7,39},{8,40},{9,... | collective-permute-start | bytes 393224 | tf_op jit(solution)/shard_map/ppermute | solution.py:418
  87.5 1.3 %collective-permute-start = (bf16[1,128,512]{2,1,0:T(8,128)(2,1)S(1)}, bf16[1,128,512]{2,1,0:T(8,128)(2,1)S(1)}, u32[]{:S(2)}, u32[]{:S(2)}) collective-permute-start(bf16[1,128,512]{2,1,0:T(8,128)(2,1)S(1)} %get-tuple-element.13.refs_1_), channel_id=1, source_target_pairs={{16,48},{17,49},{18,50},{19,51},{20,52},{21,53},{22,54},{23,55},{2... | collective-permute-start | bytes 393224 | tf_op jit(solution)/shard_map/ppermute | solution.py:417
  88.8 2.0 %all-to-all-done.1 = bf16[32,5,2,128]{3,2,1,0:T(2,128)(2,1)S(1)} async-done(((bf16[32,5,2,128]{3,2,1,0:T(2,128)(2,1)}), bf16[32,5,2,128]{3,2,1,0:T(2,128)(2,1)S(1)}, u32[]{:S(2)}, u32[]{:S(2)}) %all-to-all-start.1) | async-done | bytes 81952 | tf_op jit(solution)/shard_map/all_to_all | solution.py:403
  90.8 0.7 chip_sum.1
  91.5 3.6 %all-to-all-start.2 = ((bf16[16,5,2,128]{3,2,1,0:T(2,128)(2,1)}), bf16[16,5,2,128]{3,2,1,0:T(2,128)(2,1)S(1)}, u32[]{:S(2)}, u32[]{:S(2)}) async-start(bf16[16,5,2,128]{3,2,1,0:T(2,128)(2,1)} %bitcast.4), calls=%async_computation.2 | async-start | bytes 81920 | tf_op jit(solution)/shard_map/all_to_all | solution.py:403
  95.1 0.0 copy-start
  95.1 3.3 %input_gradient.1 = bf16[1,128,512]{2,1,0:T(8,128)(2,1)} custom-call(bf16[1,128,512]{2,1,0:T(8,128)(2,1)} %x_hbm.3, bf16[512,2048]{1,0:T(8,128)(2,1)} %win_hbm.3, bf16[128,2048]{1,0:T(8,128)(2,1)S(1)} %get-tuple-element.16.hgrad_ref, bf16[128,512]{1,0:T(8,128)(2,1)S(1)} %get-tuple-element.17.masked_ref), custom_call_target="tpu_custom_call" | custom-call | tf_op jit(solution)/shard_map/input_gradient/pallas_call | solution.py:264
  98.4 6.4 %collective-permute-done.1.refs_3_ = bf16[1,128,512]{2,1,0:T(8,128)(2,1)S(1)} collective-permute-done((bf16[1,128,512]{2,1,0:T(8,128)(2,1)S(1)}, bf16[1,128,512]{2,1,0:T(8,128)(2,1)S(1)}, u32[]{:S(2)}, u32[]{:S(2)}) %collective-permute-start.1) | collective-permute-done | bytes 131104 | tf_op jit(solution)/shard_map/ppermute | solution.py:418
  104.8 21.9 %collective-permute-done.refs_2_ = bf16[1,128,512]{2,1,0:T(8,128)(2,1)S(1)} collective-permute-done((bf16[1,128,512]{2,1,0:T(8,128)(2,1)S(1)}, bf16[1,128,512]{2,1,0:T(8,128)(2,1)S(1)}, u32[]{:S(2)}, u32[]{:S(2)}) %collective-permute-start) | collective-permute-done | bytes 131104 | tf_op jit(solution)/shard_map/ppermute | solution.py:417
  126.7 0.0 all-to-all-done.2
  126.7 0.0 copy-done
  126.7 1.2 finish.1
Async XLA Ops:
  6.3 4.9 %collective-permute-start.2 = (bf16[16,320,128]{2,1,0:T(8,128)(2,1)S(1)}, bf16[16,320,128]{2,1,0:T(8,128)(2,1)S(1)}, u32[]{:S(2)}, u32[]{:S(2)}) collective-permute-start(bf16[16,320,128]{2,1,0:T(8,128)(2,1)S(1)} %get-tuple-element.18), channel_id=1, source_target_pairs={{0,1},{1,0},{2,3},{3,2},{4,5},{5,4},{6,7},{7,6},{8,9},{9,8},{10,11... | collective-permute-start | bytes 3932168 | tf_op jit(solution)/shard_map/ppermute | solution.py:415
  39.5 51.3 %all-to-all-start.1 = ((bf16[32,5,2,128]{3,2,1,0:T(2,128)(2,1)}), bf16[32,5,2,128]{3,2,1,0:T(2,128)(2,1)S(1)}, u32[]{:S(2)}, u32[]{:S(2)}) async-start(bf16[32,5,2,128]{3,2,1,0:T(2,128)(2,1)} %bitcast.2), calls=%async_computation.1 | async-start | bytes 163840 | tf_op jit(solution)/shard_map/all_to_all | solution.py:403
  67.6 37.2 %collective-permute-start.1 = (bf16[1,128,512]{2,1,0:T(8,128)(2,1)S(1)}, bf16[1,128,512]{2,1,0:T(8,128)(2,1)S(1)}, u32[]{:S(2)}, u32[]{:S(2)}) collective-permute-start(bf16[1,128,512]{2,1,0:T(8,128)(2,1)S(1)} %get-tuple-element.13.refs_1_), channel_id=1, source_target_pairs={{0,32},{1,33},{2,34},{3,35},{4,36},{5,37},{6,38},{7,39},{8,40},{9,... | collective-permute-start | bytes 393224 | tf_op jit(solution)/shard_map/ppermute | solution.py:418
  87.5 39.1 %collective-permute-start = (bf16[1,128,512]{2,1,0:T(8,128)(2,1)S(1)}, bf16[1,128,512]{2,1,0:T(8,128)(2,1)S(1)}, u32[]{:S(2)}, u32[]{:S(2)}) collective-permute-start(bf16[1,128,512]{2,1,0:T(8,128)(2,1)S(1)} %get-tuple-element.13.refs_1_), channel_id=1, source_target_pairs={{16,48},{17,49},{18,50},{19,51},{20,52},{21,53},{22,54},{23,55},{2... | collective-permute-start | bytes 393224 | tf_op jit(solution)/shard_map/ppermute | solution.py:417
  91.5 35.2 %all-to-all-start.2 = ((bf16[16,5,2,128]{3,2,1,0:T(2,128)(2,1)}), bf16[16,5,2,128]{3,2,1,0:T(2,128)(2,1)S(1)}, u32[]{:S(2)}, u32[]{:S(2)}) async-start(bf16[16,5,2,128]{3,2,1,0:T(2,128)(2,1)} %bitcast.4), calls=%async_computation.2 | async-start | bytes 81920 | tf_op jit(solution)/shard_map/all_to_all | solution.py:403
  95.1 31.6 %copy-start = (s32[1,32,1]{1,2,0:T(1,128)S(1)}, s32[1,32,1]{1,2,0:T(1,128)}, u32[]{:S(2)}) copy-start(s32[1,32,1]{1,2,0:T(1,128)} %param.9) | copy-start | bytes 388

commit v4 on v3

--- a/solution.py
+++ b/solution.py
@@ -17,6 +17,7 @@
 CORES = 2
 ROWS = 320
 PIECE = 10
+FIRST_CHIP = 19
 epsilon = 1e-06
 f32 = jnp.float32
 bf16 = jnp.bfloat16
@@ -298,9 +299,10 @@
     for g in range(1, GROUPS):
         summed += parts_ref[g].astype(f32)
     total[...] = summed
-    for z in range(CHIPS):
-        ordered[PIECE * z : PIECE * z + 8, :] = total[8 * z : 8 * z + 8, :]
-        ordered[PIECE * z + 8 : PIECE * z + 10, :] = total[pl.ds(256 + z, 2, stride=CHIPS), :]
+    for j in range(CHIPS):
+        z = (FIRST_CHIP + j) % CHIPS
+        ordered[PIECE * j : PIECE * j + 8, :] = total[8 * z : 8 * z + 8, :]
+        ordered[PIECE * j + 8 : PIECE * j + 10, :] = total[pl.ds(256 + z, 2, stride=CHIPS), :]
     out_ref[...] = ordered[...].astype(bf16)
 
 
@@ -347,8 +349,7 @@
     scale,
     swap_ref,
     home_ref,
-    to_early_ref,
-    to_late_ref,
+    arrived_ref,
     parts_ref,
     out_ref,
     din_ref,
@@ -357,15 +358,10 @@
 ):
     position = lax.axis_index("wide")
     chosen = swap_ref[lax.rem(position, CHIPS)] == 1
-    late = (position >= CHIPS // 2) & (position < CHIPS * 3 // 2)
-
-    @pl.when(chosen & late)
+
+    @pl.when(chosen)
     def _():
-        out_ref[...] = to_late_ref[...]
-
-    @pl.when(chosen & jnp.logical_not(late))
-    def _():
-        out_ref[...] = to_early_ref[...]
+        out_ref[...] = arrived_ref[...]
 
     @pl.when(jnp.logical_not(chosen))
     def _():
@@ -380,7 +376,7 @@
         ]
 
 
-def finish(scale, swaps, home, to_early, to_late, parts):
+def finish(scale, swaps, home, arrived, parts):
     vmem = pl.BlockSpec(memory_space=pltpu.VMEM)
     smem = pl.BlockSpec(memory_space=pltpu.SMEM)
     return pl.pallas_call(
@@ -390,12 +386,12 @@
             jax.ShapeDtypeStruct((8, 4 * D), f32),
             jax.ShapeDtypeStruct((8, D), f32),
         ),
-        in_specs=[smem, vmem, vmem, vmem, vmem],
+        in_specs=[smem, vmem, vmem, vmem],
         out_specs=(vmem, vmem, vmem),
         scratch_shapes=[pltpu.VMEM((GROUPS * PIECE, 128), f32)],
         compiler_params=pltpu.CompilerParams(vmem_limit_bytes=8 << 20),
         name="finish",
-    )(swaps, *kept_in(pltpu.VMEM, home, to_early, to_late, parts))
+    )(swaps, *kept_in(pltpu.VMEM, home, arrived, parts))
 
 
 def exchanged(rows, count, axis, groups=None):
@@ -410,22 +406,22 @@
     home, send, hgrad, masked, keep_in, keep_out = layer(
         lengths.reshape(wide), sequences, upstream, input_weight, output_weight
     )
-    late = range(half // 2, half * 3 // 2)
-    route = [(i, (i + half) % wide) for i in range(wide)]
+    same_core = [
+        [2 * ((FIRST_CHIP + j) % CHIPS) + c for j in range(CHIPS)] for c in range(CORES)
+    ]
     received = lax.ppermute(send, "wide", [(i, i ^ 1) for i in range(wide)])
     keep = kept_half(keep_in, keep_out, hgrad, masked)
-    to_early = lax.ppermute(home, "wide", [r for r in route if r[0] in late])
-    to_late = lax.ppermute(home, "wide", [r for r in route if r[1] in late])
+    arrived = lax.ppermute(home, "wide", [(i, (i + half) % wide) for i in range(wide)])
     chip = chip_half(keep, received)
     parts = lax.all_to_all(chip, "grp", 0, 0, tiled=True)
     input_grad = input_gradient(sequences, input_weight, hgrad, masked)
     parts = group_sum(parts)
-    same_core = [[2 * z + c for z in range(CHIPS)] for c in range(CORES)]
     parts = exchanged(parts, CHIPS, "wide", same_core)
-    parts = exchanged(chip_sum(parts), GROUPS, "grp")
+    parts = chip_sum(parts)
+    parts = exchanged(parts, GROUPS, "grp")
     scale = 1.0 / math.sqrt(LEN * wide * lax.axis_size("grp"))
     layer_out, total_in, total_out = finish(
-        scale, swap_table.reshape(half), home, to_early, to_late, parts
+        scale, swap_table.reshape(half), home, arrived, parts
     )
     return (layer_out, input_grad, total_in, total_out)
 

time: 128 us -> 116 us (0.906)
  the two profiles are of different devices: /device:TPU:64 before, /device:TPU:65 now
where the time goes in v4:
time: 116 us
  starting transfers between devices  41 us (35%)
  waiting for transfers between devices  36 us (31%)
  blocking collectives  26 us (22%)
  Pallas kernels  12.5 us (11%)
    all_to_all x2, starting transfers between devices, exchanged(): lax.all_to_all(pieces, axis, 0, 0, tiled=True, axis_index_groups=groups)  35.2 us
    ppermute x1, waiting for transfers between devices, body(): lax.ppermute(home, 'wide', [(i, (i + half) % wide) for i in range(wide)])  29 us
    all_to_all x1, blocking collectives, body(): parts = lax.all_to_all(chip, 'grp', 0, 0, tiled=True)  26 us
    pallas_call x1, Pallas kernels, layer(): pl.pallas_call(layer_kernel, out_shape=[jax.ShapeDtypeStruct(shape, bf16)...  5.64 us
    all_to_all x2, waiting for transfers between devices, exchanged(): lax.all_to_all(pieces, axis, 0, 0, tiled=True, axis_index_groups=groups)  4.79 us
    pallas_call x1, Pallas kernels, input_gradient(): pl.pallas_call(input_grad_kernel, out_shape=jax.ShapeDtypeStruct((1, LEN,...  3.26 us
    ppermute x1, starting transfers between devices, body(): lax.ppermute(home, 'wide', [(i, (i + half) % wide) for i in range(wide)])  3.18 us
    ppermute x1, starting transfers between devices, body(): received = lax.ppermute(send, 'wide', [(i, i ^ 1) for i in range(wide)])  2.58 us
  transfers between devices with their start and end apart: 4, of which 3 were waited for; matrix products, arithmetic and copies ran while one was open for 0% of the time, Pallas kernels for 4%

profile of v4, /device:TPU:65, one launch (start us, length us, event | category | flops | bytes accessed | tf_op | source)
XLA Modules:
  0.0 116.1 jit_solution(5201918882017860654)
XLA Ops:
  0.6 5.6 %layer.1 = (bf16[1,128,512]{2,1,0:T(8,128)(2,1)S(1)}, bf16[16,320,128]{2,1,0:T(8,128)(2,1)S(1)}, bf16[128,2048]{1,0:T(8,128)(2,1)S(1)}, bf16[128,512]{1,0:T(8,12...) custom-call(s32[64]{0:T(128)} %bitcast.9, bf16[1,128,512]{2,1,0:T(8,128)(2,1)} %x_hbm.3, ...), custom_call_target="tpu_custom_call" | custom-call | tf_op jit(solution)/shard_map/layer/pallas_call | solution.py:226
  6.3 2.6 %collective-permute-start.1 = (bf16[16,320,128]{2,1,0:T(8,128)(2,1)S(1)}, bf16[16,320,128]{2,1,0:T(8,128)(2,1)S(1)}, u32[]{:S(2)}, u32[]{:S(2)}) collective-permute-start(bf16[16,320,128]{2,1,0:T(8,128)(2,1)S(1)} %get-tuple-element.18), channel_id=1, source_target_pairs={{0,1},{1,0},{2,3},{3,2},{4,5},{5,4},{6,7},{7,6},{8,9},{9,8},{10,11... | collective-permute-start | bytes 3932168 | tf_op jit(solution)/shard_map/ppermute | solution.py:412
  8.9 0.5 kept_half.1.keep_ref
  9.4 2.1 %collective-permute-done.1.received_ref = bf16[16,320,128]{2,1,0:T(8,128)(2,1)S(1)} collective-permute-done((bf16[16,320,128]{2,1,0:T(8,128)(2,1)S(1)}, bf16[16,320,128]{2,1,0:T(8,128)(2,1)S(1)}, u32[]{:S(2)}, u32[]{:S(2)}) %collective-permute-start.1) | collective-permute-done | bytes 1310752 | tf_op jit(solution)/shard_map/ppermute | solution.py:412
  11.5 0.3 chip_half.1
  11.8 26.0 %all_to_all.15.parts_ref = bf16[16,320,128]{2,1,0:T(8,128)(2,1)S(1)} all-to-all(bf16[16,320,128]{2,1,0:T(8,128)(2,1)S(1)} %chip_half.1), channel_id=1, replica_groups=mesh['grp'=16,'wide'=64] {'grp'}, dimensions={0} | all-to-all | bytes 2621440 | tf_op jit(solution)/shard_map/all_to_all | solution.py:416
  37.8 0.9 group_sum.1
  38.7 31.7 %all-to-all-start.1 = ((bf16[32,5,2,128]{3,2,1,0:T(2,128)(2,1)}), bf16[32,5,2,128]{3,2,1,0:T(2,128)(2,1)S(1)}, u32[]{:S(2)}, u32[]{:S(2)}) async-start(bf16[32,5,2,128]{3,2,1,0:T(2,128)(2,1)} %bitcast.2), calls=%async_computation.1 | async-start | bytes 163840 | tf_op jit(solution)/shard_map/all_to_all | solution.py:399
  70.4 3.2 %collective-permute-start = (bf16[1,128,512]{2,1,0:T(8,128)(2,1)S(1)}, bf16[1,128,512]{2,1,0:T(8,128)(2,1)S(1)}, u32[]{:S(2)}, u32[]{:S(2)}) collective-permute-start(bf16[1,128,512]{2,1,0:T(8,128)(2,1)S(1)} %get-tuple-element.13.refs_1_), channel_id=1, source_target_pairs={{0,32},{1,33},{2,34},{3,35},{4,36},{5,37},{6,38},{7,39},{8,40},{9,... | collective-permute-start | bytes 393224 | tf_op jit(solution)/shard_map/ppermute | solution.py:414
  73.6 4.8 %all-to-all-done.1 = bf16[32,5,2,128]{3,2,1,0:T(2,128)(2,1)S(1)} async-done(((bf16[32,5,2,128]{3,2,1,0:T(2,128)(2,1)}), bf16[32,5,2,128]{3,2,1,0:T(2,128)(2,1)S(1)}, u32[]{:S(2)}, u32[]{:S(2)}) %all-to-all-start.1) | async-done | bytes 81952 | tf_op jit(solution)/shard_map/all_to_all | solution.py:399
  78.4 0.7 chip_sum.1
  79.1 3.5 %all-to-all-start.2 = ((bf16[16,5,2,128]{3,2,1,0:T(2,128)(2,1)}), bf16[16,5,2,128]{3,2,1,0:T(2,128)(2,1)S(1)}, u32[]{:S(2)}, u32[]{:S(2)}) async-start(bf16[16,5,2,128]{3,2,1,0:T(2,128)(2,1)} %bitcast.4), calls=%async_computation.2 | async-start | bytes 81920 | tf_op jit(solution)/shard_map/all_to_all | solution.py:399
  82.6 0.0 copy-start
  82.6 3.3 %input_gradient.1 = bf16[1,128,512]{2,1,0:T(8,128)(2,1)} custom-call(bf16[1,128,512]{2,1,0:T(8,128)(2,1)} %x_hbm.3, bf16[512,2048]{1,0:T(8,128)(2,1)} %win_hbm.3, bf16[128,2048]{1,0:T(8,128)(2,1)S(1)} %get-tuple-element.16.hgrad_ref, bf16[128,512]{1,0:T(8,128)(2,1)S(1)} %get-tuple-element.17.masked_ref), custom_call_target="tpu_custom_call" | custom-call | tf_op jit(solution)/shard_map/input_gradient/pallas_call | solution.py:265
  85.8 29.0 %collective-permute-done.refs_2_ = bf16[1,128,512]{2,1,0:T(8,128)(2,1)S(1)} collective-permute-done((bf16[1,128,512]{2,1,0:T(8,128)(2,1)S(1)}, bf16[1,128,512]{2,1,0:T(8,128)(2,1)S(1)}, u32[]{:S(2)}, u32[]{:S(2)}) %collective-permute-start) | collective-permute-done | bytes 131104 | tf_op jit(solution)/shard_map/ppermute | solution.py:414
  114.9 0.0 all-to-all-done.2
  114.9 0.0 copy-done
  114.9 1.2 %finish.1 = (bf16[1,128,512]{2,1,0:T(8,128)(2,1)}, f32[8,2048]{1,0:T(8,128)}, f32[8,512]{1,0:T(8,128)}) custom-call(s32[32]{0:T(128)S(1)} %bitcast.8, bf16[1,128,512]{2,1,0:T(8,128)(2,1)S(1)} %get-tuple-element.13.refs_1_, bf16[1,128,512]{2,1,0:T(8,128)(2,1)S(1)} %collective-permute-done.refs_2_, bf16[160,128]{1,0:T(8,128)(2,1)S(1)} %bitcast.7), custom_call_target="tpu_custom_call" | custom-call | tf_op jit(solution)/shard_map/finish/pallas_call | solution.py:382
Async XLA Ops:
  6.3 5.2 %collective-permute-start.1 = (bf16[16,320,128]{2,1,0:T(8,128)(2,1)S(1)}, bf16[16,320,128]{2,1,0:T(8,128)(2,1)S(1)}, u32[]{:S(2)}, u32[]{:S(2)}) collective-permute-start(bf16[16,320,128]{2,1,0:T(8,128)(2,1)S(1)} %get-tuple-element.18), channel_id=1, source_target_pairs={{0,1},{1,0},{2,3},{3,2},{4,5},{5,4},{6,7},{7,6},{8,9},{9,8},{10,11... | collective-permute-start | bytes 3932168 | tf_op jit(solution)/shard_map/ppermute | solution.py:412
  38.7 39.7 %all-to-all-start.1 = ((bf16[32,5,2,128]{3,2,1,0:T(2,128)(2,1)}), bf16[32,5,2,128]{3,2,1,0:T(2,128)(2,1)S(1)}, u32[]{:S(2)}, u32[]{:S(2)}) async-start(bf16[32,5,2,128]{3,2,1,0:T(2,128)(2,1)} %bitcast.2), calls=%async_computation.1 | async-start | bytes 163840 | tf_op jit(solution)/shard_map/all_to_all | solution.py:399
  70.4 44.5 %collective-permute-start = (bf16[1,128,512]{2,1,0:T(8,128)(2,1)S(1)}, bf16[1,128,512]{2,1,0:T(8,128)(2,1)S(1)}, u32[]{:S(2)}, u32[]{:S(2)}) collective-permute-start(bf16[1,128,512]{2,1,0:T(8,128)(2,1)S(1)} %get-tuple-element.13.refs_1_), channel_id=1, source_target_pairs={{0,32},{1,33},{2,34},{3,35},{4,36},{5,37},{6,38},{7,39},{8,40},{9,... | collective-permute-start | bytes 393224 | tf_op jit(solution)/shard_map/ppermute | solution.py:414
  79.1 35.8 %all-to-all-start.2 = ((bf16[16,5,2,128]{3,2,1,0:T(2,128)(2,1)}), bf16[16,5,2,128]{3,2,1,0:T(2,128)(2,1)S(1)}, u32[]{:S(2)}, u32[]{:S(2)}) async-start(bf16[16,5,2,128]{3,2,1,0:T(2,128)(2,1)} %bitcast.4), calls=%async_computation.2 | async-start | bytes 81920 | tf_op jit(solution)/shard_map/all_to_all | solution.py:399
  82.6 32.3 %copy-start = (s32[1,32,1]{1,2,0:T(1,128)S(1)}, s32[1,32,1]{1,2,0:T(1,128)}, u32[]{:S(2)}) copy-start(s32[1,32,1]{1,2,0:T(1,128)} %param.9) | copy-start | bytes 388

commit v5 on v4

--- a/solution.py
+++ b/solution.py
@@ -17,7 +17,8 @@
 CORES = 2
 ROWS = 320
 PIECE = 10
-FIRST_CHIP = 19
+FIRST_CHIP = 22
+FIRST_GROUP = 10
 epsilon = 1e-06
 f32 = jnp.float32
 bf16 = jnp.bfloat16
@@ -37,17 +38,21 @@
 
 def sigmoid(x):
     return 0.5 * jnp.tanh(0.5 * x) + 0.5
+
+
+def place(group):
+    return (group - FIRST_GROUP) % GROUPS
 
 
 def store_grads(out_ref, mine_in, mine_out, hgrad_ref, masked):
     for block in range(4):
         grads = nn(mine_in, hgrad_ref[:, block * 512 : (block + 1) * 512]).astype(bf16)
         for j in range(4):
-            out_ref[4 * block + j, 0:256, :] = grads[:, j * 128 : (j + 1) * 128]
+            out_ref[place(4 * block + j), 0:256, :] = grads[:, j * 128 : (j + 1) * 128]
     grads = nn(mine_out, masked).astype(bf16)
     for block in range(4):
         for p in range(4):
-            out_ref[4 * block + p, 256:320, :] = grads[
+            out_ref[place(4 * block + p), 256:320, :] = grads[
                 p * 64 : (p + 1) * 64, block * 128 : (block + 1) * 128
             ]
 
@@ -406,6 +411,7 @@
     home, send, hgrad, masked, keep_in, keep_out = layer(
         lengths.reshape(wide), sequences, upstream, input_weight, output_weight
     )
+    plane = [[(FIRST_GROUP + j) % GROUPS for j in range(GROUPS)]]
     same_core = [
         [2 * ((FIRST_CHIP + j) % CHIPS) + c for j in range(CHIPS)] for c in range(CORES)
     ]
@@ -413,7 +419,7 @@
     keep = kept_half(keep_in, keep_out, hgrad, masked)
     arrived = lax.ppermute(home, "wide", [(i, (i + half) % wide) for i in range(wide)])
     chip = chip_half(keep, received)
-    parts = lax.all_to_all(chip, "grp", 0, 0, tiled=True)
+    parts = lax.all_to_all(chip, "grp", 0, 0, tiled=True, axis_index_groups=plane)
     input_grad = input_gradient(sequences, input_weight, hgrad, masked)
     parts = group_sum(parts)
     parts = exchanged(parts, CHIPS, "wide", same_core)

time: 116 us -> 111 us (0.957)
  the two profiles are of different devices: /device:TPU:65 before, /device:TPU:32 now
where the time goes in v5:
time: 111 us; the launch traced here: 110 us
  starting transfers between devices  46.4 us (42%)
  waiting for transfers between devices  26.7 us (24%)
  blocking collectives  23.9 us (22%)
  Pallas kernels  12.5 us (11%)
    all_to_all x2, starting transfers between devices, exchanged(): lax.all_to_all(pieces, axis, 0, 0, tiled=True, axis_index_groups=groups)  36.3 us
    all_to_all x2, waiting for transfers between devices, exchanged(): lax.all_to_all(pieces, axis, 0, 0, tiled=True, axis_index_groups=groups)  24.2 us
    all_to_all x1, blocking collectives, body(): lax.all_to_all(chip, 'grp', 0, 0, tiled=True, axis_index_groups=plane)  23.9 us
    ppermute x1, starting transfers between devices, body(): lax.ppermute(home, 'wide', [(i, (i + half) % wide) for i in range(wide)])  8.24 us
    pallas_call x1, Pallas kernels, layer(): pl.pallas_call(layer_kernel, out_shape=[jax.ShapeDtypeStruct(shape, bf16)...  5.64 us
    pallas_call x1, Pallas kernels, input_gradient(): pl.pallas_call(input_grad_kernel, out_shape=jax.ShapeDtypeStruct((1, LEN,...  3.26 us
    ppermute x1, waiting for transfers between devices, body(): received = lax.ppermute(send, 'wide', [(i, i ^ 1) for i in range(wide)])  2.5 us
  transfers between devices with their start and end apart: 4, of which 3 were waited for; matrix products, arithmetic and copies ran while one was open for 0% of the time, Pallas kernels for 4%

profile of v5, /device:TPU:32, one launch (start us, length us, event | category | flops | bytes accessed | tf_op | source)
XLA Modules:
  0.0 110.2 jit_solution(6732457181593484892)
XLA Ops:
  0.6 5.6 %layer.1 = (bf16[1,128,512]{2,1,0:T(8,128)(2,1)S(1)}, bf16[16,320,128]{2,1,0:T(8,128)(2,1)S(1)}, bf16[128,2048]{1,0:T(8,128)(2,1)S(1)}, bf16[128,512]{1,0:T(8,12...) custom-call(s32[64]{0:T(128)} %bitcast.9, bf16[1,128,512]{2,1,0:T(8,128)(2,1)} %x_hbm.3, ...), custom_call_target="tpu_custom_call" | custom-call | tf_op jit(solution)/shard_map/layer/pallas_call | solution.py:231
  6.3 1.9 %collective-permute-start.1 = (bf16[16,320,128]{2,1,0:T(8,128)(2,1)S(1)}, bf16[16,320,128]{2,1,0:T(8,128)(2,1)S(1)}, u32[]{:S(2)}, u32[]{:S(2)}) collective-permute-start(bf16[16,320,128]{2,1,0:T(8,128)(2,1)S(1)} %get-tuple-element.18), channel_id=1, source_target_pairs={{0,1},{1,0},{2,3},{3,2},{4,5},{5,4},{6,7},{7,6},{8,9},{9,8},{10,11... | collective-permute-start | bytes 3932168 | tf_op jit(solution)/shard_map/ppermute | solution.py:418
  8.2 0.5 kept_half.1.keep_ref
  8.7 2.5 %collective-permute-done.1.received_ref = bf16[16,320,128]{2,1,0:T(8,128)(2,1)S(1)} collective-permute-done((bf16[16,320,128]{2,1,0:T(8,128)(2,1)S(1)}, bf16[16,320,128]{2,1,0:T(8,128)(2,1)S(1)}, u32[]{:S(2)}, u32[]{:S(2)}) %collective-permute-start.1) | collective-permute-done | bytes 1310752 | tf_op jit(solution)/shard_map/ppermute | solution.py:418
  11.2 0.3 chip_half.1
  11.5 23.9 %all_to_all.15.parts_ref = bf16[16,320,128]{2,1,0:T(8,128)(2,1)S(1)} all-to-all(bf16[16,320,128]{2,1,0:T(8,128)(2,1)S(1)} %chip_half.1), channel_id=1, replica_groups={{640,704,768,832,896,960,0,64,128,192,256,320,384,448,512,576},{641,705..., dimensions={0} | all-to-all | bytes 2621440 | tf_op jit(solution)/shard_map/all_to_all | solution.py:422
  35.4 0.9 group_sum.1
  36.3 28.8 %all-to-all-start.1 = ((bf16[32,5,2,128]{3,2,1,0:T(2,128)(2,1)}), bf16[32,5,2,128]{3,2,1,0:T(2,128)(2,1)S(1)}, u32[]{:S(2)}, u32[]{:S(2)}) async-start(bf16[32,5,2,128]{3,2,1,0:T(2,128)(2,1)} %bitcast.2), calls=%async_computation.1 | async-start | bytes 163840 | tf_op jit(solution)/shard_map/all_to_all | solution.py:404
  65.1 8.2 %collective-permute-start = (bf16[1,128,512]{2,1,0:T(8,128)(2,1)S(1)}, bf16[1,128,512]{2,1,0:T(8,128)(2,1)S(1)}, u32[]{:S(2)}, u32[]{:S(2)}) collective-permute-start(bf16[1,128,512]{2,1,0:T(8,128)(2,1)S(1)} %get-tuple-element.13.refs_1_), channel_id=1, source_target_pairs={{0,32},{1,33},{2,34},{3,35},{4,36},{5,37},{6,38},{7,39},{8,40},{9,... | collective-permute-start | bytes 393224 | tf_op jit(solution)/shard_map/ppermute | solution.py:420
  73.3 19.9 %all-to-all-done.1 = bf16[32,5,2,128]{3,2,1,0:T(2,128)(2,1)S(1)} async-done(((bf16[32,5,2,128]{3,2,1,0:T(2,128)(2,1)}), bf16[32,5,2,128]{3,2,1,0:T(2,128)(2,1)S(1)}, u32[]{:S(2)}, u32[]{:S(2)}) %all-to-all-start.1) | async-done | bytes 81952 | tf_op jit(solution)/shard_map/all_to_all | solution.py:404
  93.2 0.7 chip_sum.1
  93.9 7.4 %all-to-all-start.2 = ((bf16[16,5,2,128]{3,2,1,0:T(2,128)(2,1)}), bf16[16,5,2,128]{3,2,1,0:T(2,128)(2,1)S(1)}, u32[]{:S(2)}, u32[]{:S(2)}) async-start(bf16[16,5,2,128]{3,2,1,0:T(2,128)(2,1)} %bitcast.4), calls=%async_computation.2 | async-start | bytes 81920 | tf_op jit(solution)/shard_map/all_to_all | solution.py:404
  101.3 0.0 copy-start
  101.3 3.3 %input_gradient.1 = bf16[1,128,512]{2,1,0:T(8,128)(2,1)} custom-call(bf16[1,128,512]{2,1,0:T(8,128)(2,1)} %x_hbm.3, bf16[512,2048]{1,0:T(8,128)(2,1)} %win_hbm.3, bf16[128,2048]{1,0:T(8,128)(2,1)S(1)} %get-tuple-element.16.hgrad_ref, bf16[128,512]{1,0:T(8,128)(2,1)S(1)} %get-tuple-element.17.masked_ref), custom_call_target="tpu_custom_call" | custom-call | tf_op jit(solution)/shard_map/input_gradient/pallas_call | solution.py:270
  104.6 0.0 collective-permute-done.refs_2_
  104.6 4.3 %all-to-all-done.2 = bf16[16,5,2,128]{3,2,1,0:T(2,128)(2,1)S(1)} async-done(((bf16[16,5,2,128]{3,2,1,0:T(2,128)(2,1)}), bf16[16,5,2,128]{3,2,1,0:T(2,128)(2,1)S(1)}, u32[]{:S(2)}, u32[]{:S(2)}) %all-to-all-start.2) | async-done | bytes 40992 | tf_op jit(solution)/shard_map/all_to_all | solution.py:404
  108.9 0.0 copy-done
  108.9 1.2 %finish.1 = (bf16[1,128,512]{2,1,0:T(8,128)(2,1)}, f32[8,2048]{1,0:T(8,128)}, f32[8,512]{1,0:T(8,128)}) custom-call(s32[32]{0:T(128)S(1)} %bitcast.8, bf16[1,128,512]{2,1,0:T(8,128)(2,1)S(1)} %get-tuple-element.13.refs_1_, bf16[1,128,512]{2,1,0:T(8,128)(2,1)S(1)} %collective-permute-done.refs_2_, bf16[160,128]{1,0:T(8,128)(2,1)S(1)} %bitcast.7), custom_call_target="tpu_custom_call" | custom-call | tf_op jit(solution)/shard_map/finish/pallas_call | solution.py:387
Async XLA Ops:
  6.3 4.9 %collective-permute-start.1 = (bf16[16,320,128]{2,1,0:T(8,128)(2,1)S(1)}, bf16[16,320,128]{2,1,0:T(8,128)(2,1)S(1)}, u32[]{:S(2)}, u32[]{:S(2)}) collective-permute-start(bf16[16,320,128]{2,1,0:T(8,128)(2,1)S(1)} %get-tuple-element.18), channel_id=1, source_target_pairs={{0,1},{1,0},{2,3},{3,2},{4,5},{5,4},{6,7},{7,6},{8,9},{9,8},{10,11... | collective-permute-start | bytes 3932168 | tf_op jit(solution)/shard_map/ppermute | solution.py:418
  36.3 56.9 %all-to-all-start.1 = ((bf16[32,5,2,128]{3,2,1,0:T(2,128)(2,1)}), bf16[32,5,2,128]{3,2,1,0:T(2,128)(2,1)S(1)}, u32[]{:S(2)}, u32[]{:S(2)}) async-start(bf16[32,5,2,128]{3,2,1,0:T(2,128)(2,1)} %bitcast.2), calls=%async_computation.1 | async-start | bytes 163840 | tf_op jit(solution)/shard_map/all_to_all | solution.py:404
  65.1 39.5 %collective-permute-start = (bf16[1,128,512]{2,1,0:T(8,128)(2,1)S(1)}, bf16[1,128,512]{2,1,0:T(8,128)(2,1)S(1)}, u32[]{:S(2)}, u32[]{:S(2)}) collective-permute-start(bf16[1,128,512]{2,1,0:T(8,128)(2,1)S(1)} %get-tuple-element.13.refs_1_), channel_id=1, source_target_pairs={{0,32},{1,33},{2,34},{3,35},{4,36},{5,37},{6,38},{7,39},{8,40},{9,... | collective-permute-start | bytes 393224 | tf_op jit(solution)/shard_map/ppermute | solution.py:420
  93.9 15.0 %all-to-all-start.2 = ((bf16[16,5,2,128]{3,2,1,0:T(2,128)(2,1)}), bf16[16,5,2,128]{3,2,1,0:T(2,128)(2,1)S(1)}, u32[]{:S(2)}, u32[]{:S(2)}) async-start(bf16[16,5,2,128]{3,2,1,0:T(2,128)(2,1)} %bitcast.4), calls=%async_computation.2 | async-start | bytes 81920 | tf_op jit(solution)/shard_map/all_to_all | solution.py:404
  101.3 7.6 %copy-start = (s32[1,32,1]{1,2,0:T(1,128)S(1)}, s32[1,32,1]{1,2,0:T(1,128)}, u32[]{:S(2)}) copy-start(s32[1,32,1]{1,2,0:T(1,128)} %param.9) | copy-start | bytes 388

commit v6 on v5

--- a/solution.py
+++ b/solution.py
@@ -44,19 +44,6 @@
     return (group - FIRST_GROUP) % GROUPS
 
 
-def store_grads(out_ref, mine_in, mine_out, hgrad_ref, masked):
-    for block in range(4):
-        grads = nn(mine_in, hgrad_ref[:, block * 512 : (block + 1) * 512]).astype(bf16)
-        for j in range(4):
-            out_ref[place(4 * block + j), 0:256, :] = grads[:, j * 128 : (j + 1) * 128]
-    grads = nn(mine_out, masked).astype(bf16)
-    for block in range(4):
-        for p in range(4):
-            out_ref[place(4 * block + p), 256:320, :] = grads[
-                p * 64 : (p + 1) * 64, block * 128 : (block + 1) * 128
-            ]
-
-
 def layer_kernel(
     lengths_hbm,
     x_hbm,
@@ -64,11 +51,8 @@
     win_hbm,
     wout_hbm,
     home_ref,
-    send_ref,
-    hgrad_ref,
-    masked_ref,
-    keep_in_ref,
-    keep_out_ref,
+    factors_ref,
+    mine_ref,
     act_ref,
     slope_ref,
     wslope_ref,
@@ -151,9 +135,9 @@
     copies[7].wait()
     alive = lax.broadcasted_iota(jnp.int32, (LEN, D), 0) < length
     masked = jnp.where(alive, up_ref[...].astype(f32), 0.0).astype(bf16)
-    masked_ref[...] = masked
+    factors_ref[:, 4 * D : 5 * D] = masked
     gated_grad = nt(masked, wout_ref[...]).astype(bf16).astype(f32)
-    hgrad_ref[:, :D] = (
+    factors_ref[:, :D] = (
         (gated_grad * unit_attended).astype(bf16).astype(f32) * slope_ref[:, :D]
     ).astype(bf16)
     unit_grad = gated_grad * gate
@@ -176,25 +160,50 @@
         key_grad = tn(score_grads, jnp.concatenate(queries, axis=0))
         for start, grad in ((D, value_grad), (2 * D, query_grad), (3 * D, key_grad)):
             columns = pl.ds(start + at, 128)
-            hgrad_ref[:, columns] = (grad * slope_ref[:, columns]).astype(bf16)
-
-    def mine(side):
+            factors_ref[:, columns] = (grad * slope_ref[:, columns]).astype(bf16)
+
+    def columns_of(side):
         rows = pl.ds(pl.multiple_of(side * 8, 8), 8)
-        mine_in = normed_t[:, rows, :].reshape(256, LEN).astype(bf16)
-        mine_out = jnp.concatenate(
+        normed_part = normed_t[:, rows, :].reshape(256, LEN).astype(bf16)
+        gated_part = jnp.concatenate(
             [gated_t[pl.ds(side * 8 + i, CHIPS, stride=16), :] for i in range(8)], axis=0
         ).astype(bf16)
-        return mine_in, mine_out
-
-    keep_in_ref[...], keep_out_ref[...] = mine(core)
-    store_grads(send_ref, *mine(1 - core), hgrad_ref, masked)
-
-
-def keep_kernel(keep_in_ref, keep_out_ref, hgrad_ref, masked_ref, keep_ref):
-    store_grads(keep_ref, keep_in_ref[...], keep_out_ref[...], hgrad_ref, masked_ref[...])
-
-
-def input_grad_kernel(x_hbm, win_hbm, hgrad_ref, masked_ref, xgrad_ref, x_ref, win_ref, arrivals):
+        return (normed_part[:128], normed_part[128:], gated_part[:128], gated_part[128:])
+
+    for i, block in enumerate(columns_of(1 - core)):
+        factors_ref[:, 5 * D + 128 * i : 5 * D + 128 * (i + 1)] = block
+    for i, block in enumerate(columns_of(core)):
+        mine_ref[128 * i : 128 * (i + 1), :] = block
+
+
+def pair_kernel(factors_ref, received_ref, mine_ref, out_hbm, out_ref, sent):
+    theirs = [received_ref[:, 5 * D + 128 * i : 5 * D + 128 * (i + 1)] for i in range(4)]
+    theirs = jnp.concatenate(theirs, axis=0)
+    left = jnp.concatenate([mine_ref[...], theirs], axis=1)
+
+    def right(start, width):
+        columns = pl.ds(start, width)
+        return jnp.concatenate([factors_ref[:, columns], received_ref[:, columns]], axis=0)
+
+    grads_out = nn(left[256:], right(4 * D, D)).astype(bf16)
+    copies = []
+    for block in range(4):
+        grads = nn(left[:256], right(block * D, D)).astype(bf16)
+        for j in range(4):
+            at = place(4 * block + j)
+            out_ref[at, 0:256, :] = grads[:, j * 128 : (j + 1) * 128]
+            out_ref[at, 256:320, :] = grads_out[
+                j * 64 : (j + 1) * 64, block * 128 : (block + 1) * 128
+            ]
+            copies.append(
+                pltpu.make_async_copy(out_ref.at[at], out_hbm.at[at], sent.at[4 * block + j])
+            )
+            copies[-1].start()
+    for copy in copies:
+        copy.wait()
+
+
+def input_grad_kernel(x_hbm, win_hbm, factors_ref, xgrad_ref, x_ref, win_ref, arrivals):
     copies = [
         pltpu.make_async_copy(x_hbm.at[0], x_ref, arrivals.at[0]),
         pltpu.make_async_copy(win_hbm, win_ref, arrivals.at[1]),
@@ -206,10 +215,10 @@
     inverse = lax.rsqrt(jnp.mean(x * x, axis=-1, keepdims=True) + epsilon)
     unit = x * inverse
     copies[1].wait()
-    unit_grad = nt(hgrad_ref[...], win_ref[...])
+    unit_grad = nt(factors_ref[:, : 4 * D], win_ref[...])
     overlap = jnp.mean(unit_grad * unit, axis=-1, keepdims=True)
     xgrad_ref[0] = (
-        masked_ref[...].astype(f32) + inverse * (unit_grad - unit * overlap)
+        factors_ref[:, 4 * D : 5 * D].astype(f32) + inverse * (unit_grad - unit * overlap)
     ).astype(bf16)
 
 
@@ -220,19 +229,12 @@
 def layer(lengths, x, up, win, wout):
     vmem = pl.BlockSpec(memory_space=pltpu.VMEM)
     hbm = pl.BlockSpec(memory_space=pltpu.HBM)
-    shapes = [
-        (1, LEN, D),
-        (GROUPS, ROWS, 128),
-        (LEN, 4 * D),
-        (LEN, D),
-        (256, LEN),
-        (256, LEN),
-    ]
+    shapes = [(1, LEN, D), (LEN, 6 * D), (512, LEN)]
     return pl.pallas_call(
         layer_kernel,
         out_shape=[jax.ShapeDtypeStruct(shape, bf16) for shape in shapes],
         in_specs=[hbm] * 5,
-        out_specs=[vmem] * 6,
+        out_specs=[vmem] * 3,
         scratch_shapes=[
             pltpu.VMEM((LEN, 4 * D), bf16),
             pltpu.VMEM((LEN, 4 * D), f32),
@@ -252,25 +254,27 @@
     )(*kept_in(pltpu.HBM, lengths, x, up, win, wout))
 
 
-def kept_half(keep_in, keep_out, hgrad, masked):
-    vmem = pl.BlockSpec(memory_space=pltpu.VMEM)
-    return pl.pallas_call(
-        keep_kernel,
-        out_shape=jax.ShapeDtypeStruct((GROUPS, ROWS, 128), bf16),
-        in_specs=[vmem] * 4,
-        out_specs=vmem,
-        compiler_params=pltpu.CompilerParams(vmem_limit_bytes=8 << 20),
-        name="kept_half",
-    )(*kept_in(pltpu.VMEM, keep_in, keep_out, hgrad, masked))
-
-
-def input_gradient(x, win, hgrad, masked):
+def pair_half(factors, received, mine):
+    vmem = pl.BlockSpec(memory_space=pltpu.VMEM)
+    shape = (GROUPS, ROWS, 128)
+    return pl.pallas_call(
+        pair_kernel,
+        out_shape=jax.ShapeDtypeStruct(shape, bf16),
+        in_specs=[vmem] * 3,
+        out_specs=pl.BlockSpec(memory_space=pltpu.HBM),
+        scratch_shapes=[pltpu.VMEM(shape, bf16), pltpu.SemaphoreType.DMA((GROUPS,))],
+        compiler_params=pltpu.CompilerParams(vmem_limit_bytes=12 << 20),
+        name="pair_half",
+    )(*kept_in(pltpu.VMEM, factors, received, mine))
+
+
+def input_gradient(x, win, factors):
     vmem = pl.BlockSpec(memory_space=pltpu.VMEM)
     hbm = pl.BlockSpec(memory_space=pltpu.HBM)
     return pl.pallas_call(
         input_grad_kernel,
         out_shape=jax.ShapeDtypeStruct((1, LEN, D), bf16),
-        in_specs=[hbm, hbm, vmem, vmem],
+        in_specs=[hbm, hbm, vmem],
         out_specs=vmem,
         scratch_shapes=[
             pltpu.VMEM((LEN, D), bf16),
@@ -279,24 +283,7 @@
         ],
         compiler_params=pltpu.CompilerParams(vmem_limit_bytes=8 << 20),
         name="input_gradient",
-    )(*kept_in(pltpu.HBM, x, win), *kept_in(pltpu.VMEM, hgrad, masked))
-
-
-def chip_half_kernel(keep_ref, received_ref, out_ref):
-    for g in range(GROUPS):
-        out_ref[g] = (keep_ref[g].astype(f32) + received_ref[g].astype(f32)).astype(bf16)
-
-
-def chip_half(keep, received):
-    vmem = pl.BlockSpec(memory_space=pltpu.VMEM)
-    return pl.pallas_call(
-        chip_half_kernel,
-        out_shape=jax.ShapeDtypeStruct((GROUPS, ROWS, 128), bf16),
-        in_specs=[vmem, vmem],
-        out_specs=vmem,
-        compiler_params=pltpu.CompilerParams(vmem_limit_bytes=8 << 20),
-        name="chip_half",
-    )(*kept_in(pltpu.VMEM, keep, received))
+    )(*kept_in(pltpu.HBM, x, win), *kept_in(pltpu.VMEM, factors))
 
 
 def group_sum_kernel(parts_ref, out_ref, total, ordered):
@@ -408,19 +395,18 @@
 def body(sequences, upstream, lengths, swap_table, input_weight, output_weight):
     wide = lax.axis_size("wide")
     half = wide // 2
-    home, send, hgrad, masked, keep_in, keep_out = layer(
+    home, factors, mine = layer(
         lengths.reshape(wide), sequences, upstream, input_weight, output_weight
     )
     plane = [[(FIRST_GROUP + j) % GROUPS for j in range(GROUPS)]]
     same_core = [
         [2 * ((FIRST_CHIP + j) % CHIPS) + c for j in range(CHIPS)] for c in range(CORES)
     ]
-    received = lax.ppermute(send, "wide", [(i, i ^ 1) for i in range(wide)])
-    keep = kept_half(keep_in, keep_out, hgrad, masked)
+    received = lax.ppermute(factors, "wide", [(i, i ^ 1) for i in range(wide)])
     arrived = lax.ppermute(home, "wide", [(i, (i + half) % wide) for i in range(wide)])
-    chip = chip_half(keep, received)
+    chip = pair_half(factors, received, mine)
     parts = lax.all_to_all(chip, "grp", 0, 0, tiled=True, axis_index_groups=plane)
-    input_grad = input_gradient(sequences, input_weight, hgrad, masked)
+    input_grad = input_gradient(sequences, input_weight, factors)
     parts = group_sum(parts)
     parts = exchanged(parts, CHIPS, "wide", same_core)
     parts = chip_sum(parts)

time: 111 us -> 112 us (level)
  Pallas kernels: 12.5 us -> 14.3 us
    pallas_call x2 -> x1, Pallas kernels: 0.79 us -> 2.92 us  [pair_half(): pl.pallas_call(pair_kernel, out_shape=jax.ShapeDtypeStruct(shape, bf16),...]
where the time goes in v6:
time: 112 us
  starting transfers between devices  46.8 us (42%)
  waiting for transfers between devices  26.4 us (24%)
  blocking collectives  23.9 us (21%)
  Pallas kernels  14.3 us (13%)
    all_to_all x2, starting transfers between devices, exchanged(): lax.all_to_all(pieces, axis, 0, 0, tiled=True, axis_index_groups=groups)  36.6 us
    all_to_all x2, waiting for transfers between devices, exchanged(): lax.all_to_all(pieces, axis, 0, 0, tiled=True, axis_index_groups=groups)  24.2 us
    all_to_all x1, blocking collectives, body(): lax.all_to_all(chip, 'grp', 0, 0, tiled=True, axis_index_groups=plane)  23.9 us
    ppermute x1, starting transfers between devices, body(): lax.ppermute(home, 'wide', [(i, (i + half) % wide) for i in range(wide)])  8.24 us
    pallas_call x1, Pallas kernels, layer(): pl.pallas_call(layer_kernel, out_shape=[jax.ShapeDtypeStruct(shape, bf16)...  5.33 us
    pallas_call x1, Pallas kernels, input_gradient(): pl.pallas_call(input_grad_kernel, out_shape=jax.ShapeDtypeStruct((1, LEN,...  3.26 us
    pallas_call x1, Pallas kernels, pair_half(): pl.pallas_call(pair_kernel, out_shape=jax.ShapeDtypeStruct(shape, bf16),...  2.92 us
    ppermute x1, waiting for transfers between devices, body(): received = lax.ppermute(factors, 'wide', [(i, i ^ 1) for i in range(wide)])  2.25 us
  transfers between devices with their start and end apart: 4, of which 3 were waited for; matrix products, arithmetic and copies ran while one was open for 0% of the time, Pallas kernels for 4%

profile of v6, /device:TPU:32, one launch (start us, length us, event | category | flops | bytes accessed | tf_op | source)
XLA Modules:
  0.0 112.1 jit_solution(12270529267896665048)
XLA Ops:
  0.6 5.3 %layer.1 = (bf16[1,128,512]{2,1,0:T(8,128)(2,1)S(1)}, bf16[128,3072]{1,0:T(8,128)(2,1)S(1)}, bf16[512,128]{1,0:T(8,128)(2,1)S(1)}) custom-call(s32[64]{0:T(128)} %bitcast.9, bf16[1,128,512]{2,1,0:T(8,128)(2,1)} %x_hbm.3, bf16[1,128,512]{2,1,0:T(8,128)(2,1)} %up_hbm.1, bf16[512,2048]{1,0:T(8,128)(2,1)} %win_hbm.3, bf16[512,512]{1,0:T(8,128)(2,1)} %wout_hbm.1), custom_call_target="tpu_custom_call" | custom-call | tf_op jit(solution)/shard_map/layer/pallas_call | solution.py:233
  6.0 1.9 %collective-permute-start.1 = (bf16[128,3072]{1,0:T(8,128)(2,1)S(1)}, bf16[128,3072]{1,0:T(8,128)(2,1)S(1)}, u32[]{:S(2)}, u32[]{:S(2)}) collective-permute-start(bf16[128,3072]{1,0:T(8,128)(2,1)S(1)} %get-tuple-element.11.factors_ref), channel_id=1, source_target_pairs={{0,1},{1,0},{2,3},{3,2},{4,5},{5,4},{6,7},{7,6},{8,9},{9,8},{10,11... | collective-permute-start | bytes 2359304 | tf_op jit(solution)/shard_map/ppermute | solution.py:405
  7.9 2.3 %collective-permute-done.1.received_ref = bf16[128,3072]{1,0:T(8,128)(2,1)S(1)} collective-permute-done((bf16[128,3072]{1,0:T(8,128)(2,1)S(1)}, bf16[128,3072]{1,0:T(8,128)(2,1)S(1)}, u32[]{:S(2)}, u32[]{:S(2)}) %collective-permute-start.1) | collective-permute-done | bytes 786464 | tf_op jit(solution)/shard_map/ppermute | solution.py:405
  10.1 2.9 %pair_half.1 = bf16[16,320,128]{2,1,0:T(8,128)(2,1)S(1)} custom-call(bf16[128,3072]{1,0:T(8,128)(2,1)S(1)} %get-tuple-element.11.factors_ref, bf16[128,3072]{1,0:T(8,128)(2,1)S(1)} %collective-permute-done.1.received_ref, bf16[512,128]{1,0:T(8,128)(2,1)S(1)} %get-tuple-element.12.mine_ref), custom_call_target="tpu_custom_call" | custom-call | tf_op jit(solution)/shard_map/pair_half/pallas_call | solution.py:260
  13.1 23.9 %all_to_all.15.parts_ref = bf16[16,320,128]{2,1,0:T(8,128)(2,1)S(1)} all-to-all(bf16[16,320,128]{2,1,0:T(8,128)(2,1)S(1)} %pair_half.1), channel_id=1, replica_groups={{640,704,768,832,896,960,0,64,128,192,256,320,384,448,512,576},{641,705..., dimensions={0} | all-to-all | bytes 2621440 | tf_op jit(solution)/shard_map/all_to_all | solution.py:408
  37.0 0.9 group_sum.1
  37.8 28.8 %all-to-all-start.1 = ((bf16[32,5,2,128]{3,2,1,0:T(2,128)(2,1)}), bf16[32,5,2,128]{3,2,1,0:T(2,128)(2,1)S(1)}, u32[]{:S(2)}, u32[]{:S(2)}) async-start(bf16[32,5,2,128]{3,2,1,0:T(2,128)(2,1)} %bitcast.2), calls=%async_computation.1 | async-start | bytes 163840 | tf_op jit(solution)/shard_map/all_to_all | solution.py:391
  66.7 8.2 %collective-permute-start = (bf16[1,128,512]{2,1,0:T(8,128)(2,1)S(1)}, bf16[1,128,512]{2,1,0:T(8,128)(2,1)S(1)}, u32[]{:S(2)}, u32[]{:S(2)}) collective-permute-start(bf16[1,128,512]{2,1,0:T(8,128)(2,1)S(1)} %get-tuple-element.10.refs_1_), channel_id=1, source_target_pairs={{0,32},{1,33},{2,34},{3,35},{4,36},{5,37},{6,38},{7,39},{8,40},{9,... | collective-permute-start | bytes 393224 | tf_op jit(solution)/shard_map/ppermute | solution.py:406
  74.9 19.9 %all-to-all-done.1 = bf16[32,5,2,128]{3,2,1,0:T(2,128)(2,1)S(1)} async-done(((bf16[32,5,2,128]{3,2,1,0:T(2,128)(2,1)}), bf16[32,5,2,128]{3,2,1,0:T(2,128)(2,1)S(1)}, u32[]{:S(2)}, u32[]{:S(2)}) %all-to-all-start.1) | async-done | bytes 81952 | tf_op jit(solution)/shard_map/all_to_all | solution.py:391
  94.7 0.7 chip_sum.1
  95.4 7.8 %all-to-all-start.2 = ((bf16[16,5,2,128]{3,2,1,0:T(2,128)(2,1)}), bf16[16,5,2,128]{3,2,1,0:T(2,128)(2,1)S(1)}, u32[]{:S(2)}, u32[]{:S(2)}) async-start(bf16[16,5,2,128]{3,2,1,0:T(2,128)(2,1)} %bitcast.4), calls=%async_computation.2 | async-start | bytes 81920 | tf_op jit(solution)/shard_map/all_to_all | solution.py:391
  103.2 0.0 copy-start
  103.2 3.3 %input_gradient.1 = bf16[1,128,512]{2,1,0:T(8,128)(2,1)} custom-call(bf16[1,128,512]{2,1,0:T(8,128)(2,1)} %x_hbm.3, bf16[512,2048]{1,0:T(8,128)(2,1)} %win_hbm.3, bf16[128,3072]{1,0:T(8,128)(2,1)S(1)} %get-tuple-element.11.factors_ref), custom_call_target="tpu_custom_call" | custom-call | tf_op jit(solution)/shard_map/input_gradient/pallas_call | solution.py:274
  106.5 0.0 collective-permute-done.refs_2_
  106.5 4.3 %all-to-all-done.2 = bf16[16,5,2,128]{3,2,1,0:T(2,128)(2,1)S(1)} async-done(((bf16[16,5,2,128]{3,2,1,0:T(2,128)(2,1)}), bf16[16,5,2,128]{3,2,1,0:T(2,128)(2,1)S(1)}, u32[]{:S(2)}, u32[]{:S(2)}) %all-to-all-start.2) | async-done | bytes 40992 | tf_op jit(solution)/shard_map/all_to_all | solution.py:391
  110.8 0.0 copy-done
  110.8 1.2 %finish.1 = (bf16[1,128,512]{2,1,0:T(8,128)(2,1)}, f32[8,2048]{1,0:T(8,128)}, f32[8,512]{1,0:T(8,128)}) custom-call(s32[32]{0:T(128)S(1)} %bitcast.8, bf16[1,128,512]{2,1,0:T(8,128)(2,1)S(1)} %get-tuple-element.10.refs_1_, bf16[1,128,512]{2,1,0:T(8,128)(2,1)S(1)} %collective-permute-done.refs_2_, bf16[160,128]{1,0:T(8,128)(2,1)S(1)} %bitcast.7), custom_call_target="tpu_custom_call" | custom-call | tf_op jit(solution)/shard_map/finish/pallas_call | solution.py:374
Async XLA Ops:
  6.0 4.2 %collective-permute-start.1 = (bf16[128,3072]{1,0:T(8,128)(2,1)S(1)}, bf16[128,3072]{1,0:T(8,128)(2,1)S(1)}, u32[]{:S(2)}, u32[]{:S(2)}) collective-permute-start(bf16[128,3072]{1,0:T(8,128)(2,1)S(1)} %get-tuple-element.11.factors_ref), channel_id=1, source_target_pairs={{0,1},{1,0},{2,3},{3,2},{4,5},{5,4},{6,7},{7,6},{8,9},{9,8},{10,11... | collective-permute-start | bytes 2359304 | tf_op jit(solution)/shard_map/ppermute | solution.py:405
  37.8 56.9 %all-to-all-start.1 = ((bf16[32,5,2,128]{3,2,1,0:T(2,128)(2,1)}), bf16[32,5,2,128]{3,2,1,0:T(2,128)(2,1)S(1)}, u32[]{:S(2)}, u32[]{:S(2)}) async-start(bf16[32,5,2,128]{3,2,1,0:T(2,128)(2,1)} %bitcast.2), calls=%async_computation.1 | async-start | bytes 163840 | tf_op jit(solution)/shard_map/all_to_all | solution.py:391
  66.7 39.9 %collective-permute-start = (bf16[1,128,512]{2,1,0:T(8,128)(2,1)S(1)}, bf16[1,128,512]{2,1,0:T(8,128)(2,1)S(1)}, u32[]{:S(2)}, u32[]{:S(2)}) collective-permute-start(bf16[1,128,512]{2,1,0:T(8,128)(2,1)S(1)} %get-tuple-element.10.refs_1_), channel_id=1, source_target_pairs={{0,32},{1,33},{2,34},{3,35},{4,36},{5,37},{6,38},{7,39},{8,40},{9,... | collective-permute-start | bytes 393224 | tf_op jit(solution)/shard_map/ppermute | solution.py:406
  95.4 15.4 %all-to-all-start.2 = ((bf16[16,5,2,128]{3,2,1,0:T(2,128)(2,1)}), bf16[16,5,2,128]{3,2,1,0:T(2,128)(2,1)S(1)}, u32[]{:S(2)}, u32[]{:S(2)}) async-start(bf16[16,5,2,128]{3,2,1,0:T(2,128)(2,1)} %bitcast.4), calls=%async_computation.2 | async-start | bytes 81920 | tf_op jit(solution)/shard_map/all_to_all | solution.py:391
  103.2 7.6 %copy-start = (s32[1,32,1]{1,2,0:T(1,128)S(1)}, s32[1,32,1]{1,2,0:T(1,128)}, u32[]{:S(2)}) copy-start(s32[1,32,1]{1,2,0:T(1,128)} %param.9) | copy-start | bytes 388
